TPU v7x, 256 devices: a whole 4x4x8 slice. The times are simulated.
256 devices in a mesh: row: 8 (over y, z_lo), col: 32 (over x, z_hi, core).
Axes of the slice: x: 4, y: 4, z: 8 (z_hi: 4, z_lo: 2; z = z_hi * 2 + z_lo), core: 2. Of those that a mesh axis runs over, the one named last changes fastest.
Arguments:
- latent: bfloat16 [2, 512, 256, 320], P(None, 'row', 'col'), may hold values from -28 to 28
- timestep: int32 [2], replicated, may hold values from 0 to 999
- group_norm_gain: float32 [320], replicated, may hold values from 0.5 to 1.5
- group_norm_bias: float32 [320], replicated, may hold values from -0.5 to 0.5
- conv_w: bfloat16 [3, 3, 320, 320], replicated, may hold values from -0.109375 to 0.109375
- conv_b: float32 [320], replicated, may hold values from -0.5 to 0.5
- embed_in: bfloat16 [320, 1280], replicated, may hold values from -0.3125 to 0.3125
- embed_out: bfloat16 [1280, 1280], replicated, may hold values from -0.15625 to 0.15625
- time_w: bfloat16 [1280, 320], replicated, may hold values from -0.15625 to 0.15625
- cotangent: bfloat16 [2, 512, 256, 320], P(None, 'row', 'col'), may hold values from -6 to 6
Outputs:
- block_out: bfloat16 [2, 512, 256, 320], P(None, 'row', 'col')
- input_grad: float32 [2, 512, 256, 320], P(None, 'row', 'col')
- conv_w_grad: float32 [320, 3, 3, 320], P('row')
- gain_grad: float32 [320], replicated
- bias_grad: float32 [320], replicated
- conv_b_grad: float32 [320], replicated
- time_w_grad: float32 [1280, 320], replicated
All inputs are finite; a program needn't handle non-finite values.
Results may differ from a plain program's by a relative error of at most 0.0055.
Values may be sent and summed in bfloat16 or wider, within the bound.
A program may use at most 128 MiB of HBM per device.

v0:
```python
import functools
import math

import jax
import jax.numpy as jnp
from jax import lax
from jax.sharding import Mesh
from jax.sharding import PartitionSpec as P

NORM_GROUPS = 32
ROW = ("row_0", "row_1")
COL = ("col_0", "col_1", "col_2")
ROW_COL = ("row_0", "row_1", "col_0", "col_1", "col_2")


EPS = 1e-05


def one_axis_at_a_time(shard, axes):
    return functools.reduce(lax.psum, axes, shard)


def with_halo(shard, sides, width):
    for axis, dim in sides:
        devices, length = (lax.axis_size(axis), shard.shape[dim])
        up = [(i, (i + 1) % devices) for i in range(devices - 1)]
        down = [(j, i) for i, j in up]
        last = lax.slice_in_dim(shard, length - width, length, axis=dim)
        first = lax.slice_in_dim(shard, 0, width, axis=dim)
        before = lax.ppermute(last, axis, up)
        after = lax.ppermute(first, axis, down)
        shard = jnp.concatenate([before, shard, after], axis=dim)
    return shard


def embed(timestep, embed_in, embed_out):
    half = embed_in.shape[0] // 2
    freqs = jnp.exp(-math.log(10000.0) * jnp.arange(half, dtype=jnp.float32) / half)
    angles = timestep.astype(jnp.float32)[:, None] * freqs[None, :]
    sinus = jnp.concatenate([jnp.cos(angles), jnp.sin(angles)], axis=1).astype(jnp.bfloat16)
    first_hidden = jax.nn.silu(jnp.dot(sinus, embed_in, preferred_element_type=jnp.float32)).astype(
        jnp.bfloat16
    )
    return jax.nn.silu(jnp.dot(first_hidden, embed_out, preferred_element_type=jnp.float32)).astype(
        jnp.bfloat16
    )


def local(
    latent,
    timestep,
    group_norm_gain,
    group_norm_bias,
    conv_w,
    conv_b,
    embed_in,
    embed_out,
    time_w,
    cotangent,
):
    batch_images, row_count, column_count, channel_count = latent.shape
    channels_per_group = channel_count // NORM_GROUPS
    total_rows = row_count * lax.axis_size(ROW)
    total_cols = column_count * lax.axis_size(COL)
    count = total_rows * total_cols * channels_per_group
    scale = 1.0 / math.sqrt(batch_images * total_rows * total_cols)
    x = latent.astype(jnp.float32)
    grouped = x.reshape(batch_images, row_count, column_count, NORM_GROUPS, channels_per_group)
    first_sum, second_sum = (
        one_axis_at_a_time(jnp.sum(grouped, axis=(1, 2, 4)), ROW_COL),
        one_axis_at_a_time(jnp.sum(grouped * grouped, axis=(1, 2, 4)), ROW_COL),
    )
    mean = first_sum / count
    var = second_sum / count - mean * mean
    group_centered = grouped - mean[:, None, None, :, None]
    inverse_deviation = lax.rsqrt(var + EPS)
    input_standardized = (group_centered * inverse_deviation[:, None, None, :, None]).reshape(
        batch_images, row_count, column_count, channel_count
    )
    normed_output = input_standardized * group_norm_gain + group_norm_bias
    acts = jax.nn.silu(normed_output).astype(jnp.bfloat16)
    padded = with_halo(acts, ((ROW, 1), (COL, 2)), 1)
    conv = jnp.zeros((batch_images, row_count, column_count, channel_count), jnp.float32)
    for kh in range(3):
        for kw in range(3):
            conv = conv + jnp.einsum(
                "bhwc,cd->bhwd",
                padded[:, kh : kh + row_count, kw : kw + column_count],
                conv_w[kh, kw],
                preferred_element_type=jnp.float32,
            )
    emb = embed(timestep, embed_in, embed_out)
    temb = jnp.dot(emb, time_w, preferred_element_type=jnp.float32)
    block_out = (x + conv + conv_b + temb[:, None, None, :]).astype(jnp.bfloat16)
    gpad = with_halo(cotangent, ((ROW, 1), (COL, 2)), 1)
    dacts = jnp.zeros((batch_images, row_count, column_count, channel_count), jnp.float32)
    for kh in range(3):
        for kw in range(3):
            dacts = dacts + jnp.einsum(
                "bhwd,cd->bhwc",
                gpad[:, 2 - kh : 2 - kh + row_count, 2 - kw : 2 - kw + column_count],
                conv_w[kh, kw],
                preferred_element_type=jnp.float32,
            )
    share = channel_count // lax.axis_size(ROW)
    pieces = []
    for kh in range(3):
        for kw in range(3):
            pieces.append(
                jnp.einsum(
                    "bhwc,bhwd->dc",
                    padded[:, kh : kh + row_count, kw : kw + column_count],
                    cotangent,
                    preferred_element_type=jnp.float32,
                )
            )
    summed = lax.psum(
        jnp.stack(pieces, axis=1).reshape(channel_count, 3, 3, channel_count) * scale, ROW_COL
    )
    conv_w_grad = lax.dynamic_slice_in_dim(summed, lax.axis_index(ROW) * share, share, 0)
    sig = jax.nn.sigmoid(normed_output)
    normed_gradient = dacts * sig * (1.0 + normed_output * (1.0 - sig))
    grad = cotangent.astype(jnp.float32)
    first, second_moment, gsum = (
        one_axis_at_a_time(jnp.sum(normed_gradient, axis=(1, 2)), ROW_COL),
        one_axis_at_a_time(jnp.sum(normed_gradient * input_standardized, axis=(1, 2)), ROW_COL),
        one_axis_at_a_time(jnp.sum(grad, axis=(1, 2)), ROW_COL),
    )
    m_one = (
        jnp.sum(
            (group_norm_gain * first).reshape(batch_images, NORM_GROUPS, channels_per_group), axis=2
        )
        / count
    )
    m_two = (
        jnp.sum(
            (group_norm_gain * second_moment).reshape(
                batch_images, NORM_GROUPS, channels_per_group
            ),
            axis=2,
        )
        / count
    )
    dxhat = (normed_gradient * group_norm_gain).reshape(
        batch_images, row_count, column_count, NORM_GROUPS, channels_per_group
    )
    input_grouped = input_standardized.reshape(
        batch_images, row_count, column_count, NORM_GROUPS, channels_per_group
    )
    dx = inverse_deviation[:, None, None, :, None] * (
        dxhat - m_one[:, None, None, :, None] - input_grouped * m_two[:, None, None, :, None]
    )
    input_grad = grad + dx.reshape(batch_images, row_count, column_count, channel_count)
    gain_grad = jnp.sum(second_moment, axis=0) * scale
    bias_grad = jnp.sum(first, axis=0) * scale
    conv_b_grad = jnp.sum(gsum, axis=0) * scale
    time_w_grad = jnp.dot(emb.astype(jnp.float32).T, gsum) * scale
    return (block_out, input_grad, conv_w_grad, gain_grad, bias_grad, conv_b_grad, time_w_grad)


def solution(mesh):
    finer = Mesh(mesh.devices.reshape(4, 2, 4, 4, 2), ("row_0", "row_1", "col_0", "col_1", "col_2"))
    in_specs = (
        P(None, ROW, COL, None),
        P(),
        P(),
        P(),
        P(),
        P(),
        P(),
        P(),
        P(),
        P(None, ROW, COL, None),
    )
    out_specs = (
        P(None, ROW, COL, None),
        P(None, ROW, COL, None),
        P(ROW, None, None, None),
        P(),
        P(),
        P(),
        P(),
    )
    return jax.shard_map(local, mesh=finer, in_specs=in_specs, out_specs=out_specs, check_vma=False)
```

profile of v0, /device:TPU:1, one launch (start us, length us, event | category | flops | bytes accessed | tf_op | source)
XLA Modules:
  0.0 452.7 jit_solution(7791203687677311444)
XLA Ops:
  7.2 0.9 fusion.168
  8.1 4.5 collective-permute-start.4
  12.6 1.3 collective-permute-start.5
  13.9 1.4 convert_reduce_fusion
  15.7 3.0 fusion.84
  18.7 10.1 %all-reduce.5 = (f32[2,32]{1,0:T(2,128)S(1)}, f32[2,32]{1,0:T(2,128)S(1)}) all-reduce(f32[2,32]{1,0:T(2,128)S(1)} %reduce_sum.109, f32[2,32]{1,0:T(2,128)S(1)} %reduce_sum.106), channel_id=1, replica_groups=mesh['row_0'=4,'row_1'=2,'col_0'=4,'col_1'=4,'col_2'=2] {'row_0'}, use_global_device_ids=true, to_apply=%region_9.0 | all-reduce | flops 128 | bytes 1024 | tf_op jit(solution)/shard_map/psum | solution.py:20
  28.8 3.8 all-reduce.9
  32.5 8.4 %all-reduce.3 = (f32[2,32]{1,0:T(2,128)S(1)}, f32[2,32]{1,0:T(2,128)S(1)}) all-reduce(f32[2,32]{1,0:T(2,128)S(1)} %get-tuple-element.34, f32[2,32]{1,0:T(2,128)S(1)} %get-tuple-element.35), channel_id=1, replica_groups=mesh['row_0'=4,'row_1'=2,'col_0'=4,'col_1'=4,'col_2'=2] {'col_0'}, use_global_device_ids=true, to_apply=%region_11.0 | all-reduce | flops 128 | bytes 1024 | tf_op jit(solution)/shard_map/psum | solution.py:20
  41.0 12.9 %all-reduce.1 = (f32[2,32]{1,0:T(2,128)S(1)}, f32[2,32]{1,0:T(2,128)S(1)}) all-reduce(f32[2,32]{1,0:T(2,128)S(1)} %get-tuple-element.19, f32[2,32]{1,0:T(2,128)S(1)} %get-tuple-element.20), channel_id=1, replica_groups=mesh['row_0'=4,'row_1'=2,'col_0'=4,'col_1'=4,'col_2'=2] {'col_1'}, use_global_device_ids=true, to_apply=%region_12.13 | all-reduce | flops 128 | bytes 1024 | tf_op jit(solution)/shard_map/psum | solution.py:20
  53.9 10.6 %all-reduce.7 = (f32[2,32]{1,0:T(2,128)S(1)}, f32[2,32]{1,0:T(2,128)S(1)}) all-reduce(f32[2,32]{1,0:T(2,128)S(1)} %get-tuple-element.14, f32[2,32]{1,0:T(2,128)S(1)} %get-tuple-element.15), channel_id=1, replica_groups=mesh['row_0'=4,'row_1'=2,'col_0'=4,'col_1'=4,'col_2'=2] {'col_2'}, use_global_device_ids=true, to_apply=%region_13.14 | all-reduce | flops 128 | bytes 1024 | tf_op jit(solution)/shard_map/psum | solution.py:20
  64.5 2.0 fusion.127
  66.5 1.5 fusion.172
  68.0 1.5 convert_reduce_fusion.1
  70.4 2.1 collective-permute-start.7
  72.5 2.2 collective-permute-start.6
  74.8 0.6 fusion.42
  75.4 0.6 fusion.38
  76.1 6.1 %collective-permute-done.6 = bf16[2,66,1,320]{3,2,1,0:T(2,128)(2,1)S(1)} collective-permute-done((bf16[2,66,1,320]{3,2,1,0:T(2,128)(2,1)S(1)}, bf16[2,66,1,320]{3,2,1,0:T(2,128)(2,1)S(1)}, u32[]{:S(2)}, u32[]{:S(2)}) %collective-permute-start.6) | collective-permute-done | bytes 84512 | tf_op jit(solution)/shard_map/ppermute | solution.py:31
  82.2 0.7 fusion.60
  82.9 0.7 fusion.53
  83.5 0.7 fusion.47
  84.2 0.7 fusion.50
  84.9 1.8 fusion.56
  86.7 4.0 fusion.164
  90.7 6.2 %all-reduce.4 = (f32[2,320]{1,0:T(2,128)S(1)}, f32[2,320]{1,0:T(2,128)S(1)}, f32[2,320]{1,0:T(2,128)S(1)}) all-reduce(f32[2,320]{1,0:T(2,128)S(1)} %get-tuple-element.8, f32[2,320]{1,0:T(2,128)S(1)} %get-tuple-element.7, ...), channel_id=1, replica_groups=mesh['row_0'=4,'row_1'=2,'col_0'=4,'col_1'=4,'col_2'=2] {'row_0'}, use_global_device_ids=true, to_apply=%region_22.23 | all-reduce | flops 1920 | bytes 15360 | tf_op jit(solution)/shard_map/psum | solution.py:20
  96.9 3.9 all-reduce.8
  100.8 6.2 %all-reduce.2 = (f32[2,320]{1,0:T(2,128)S(1)}, f32[2,320]{1,0:T(2,128)S(1)}, f32[2,320]{1,0:T(2,128)S(1)}) all-reduce(f32[2,320]{1,0:T(2,128)S(1)} %get-tuple-element.31, f32[2,320]{1,0:T(2,128)S(1)} %get-tuple-element.32, ...), channel_id=1, replica_groups=mesh['row_0'=4,'row_1'=2,'col_0'=4,'col_1'=4,'col_2'=2] {'col_0'}, use_global_device_ids=true, to_apply=%region_24.25 | all-reduce | flops 1920 | bytes 15360 | tf_op jit(solution)/shard_map/psum | solution.py:20
  107.0 13.2 %all-reduce = (f32[2,320]{1,0:T(2,128)S(1)}, f32[2,320]{1,0:T(2,128)S(1)}, f32[2,320]{1,0:T(2,128)S(1)}) all-reduce(f32[2,320]{1,0:T(2,128)S(1)} %get-tuple-element.16, f32[2,320]{1,0:T(2,128)S(1)} %get-tuple-element.17, f32[2,320]{1,0:T(2,128)S(1)} %get-tuple-element.18), channel_id=1, replica_groups=mesh['row_0'=4,'row_1'=2,'col_0'=4,'col_1'=4,'col_2'=2] {'col_1'}, use_global_device_ids=true, to_apply=%region_25.26 | all-reduce | flops 1920 | bytes 15360 | tf_op jit(solution)/shard_map/psum | solution.py:20
  120.2 5.0 %all-reduce.6 = (f32[2,320]{1,0:T(2,128)S(1)}, f32[2,320]{1,0:T(2,128)S(1)}, f32[2,320]{1,0:T(2,128)S(1)}) all-reduce(f32[2,320]{1,0:T(2,128)S(1)} %get-tuple-element.11, f32[2,320]{1,0:T(2,128)S(1)} %get-tuple-element.12, ...), channel_id=1, replica_groups=mesh['row_0'=4,'row_1'=2,'col_0'=4,'col_1'=4,'col_2'=2] {'col_2'}, use_global_device_ids=true, to_apply=%region_26.27 | all-reduce | flops 1920 | bytes 15360 | tf_op jit(solution)/shard_map/psum | solution.py:20
  126.0 3.5 convert_add_fusion.1
  129.5 3.0 fusion.86
  132.4 1.6 convolution_multiply_fusion
  134.0 1.3 collective-permute-start.1
  135.3 4.0 collective-permute-start
  139.3 0.6 broadcast_multiply_fusion.5
  139.9 0.6 broadcast_multiply_fusion.4
  140.5 0.6 broadcast_multiply_fusion.3
  141.1 0.3 pad_maximum_fusion.9
  141.4 2.8 collective-permute-start.3
  144.2 4.3 collective-permute-start.2
  148.5 2.8 fusion.34
  151.3 2.7 fusion.30
  154.2 2.4 pad_maximum_fusion
  156.6 3.0 fusion.79
  159.9 0.9 copy-done.7
  160.8 0.5 fusion.29
  161.6 0.5 fusion.28
  162.1 0.5 fusion.27
  162.7 0.5 fusion.26
  163.2 0.6 copy-done.5
  163.8 0.5 fusion.25
  164.4 0.5 fusion.24
  164.9 0.5 fusion.23
  165.4 0.5 fusion.22
  166.0 0.5 fusion.21
  166.5 2.4 broadcast_multiply_fusion
  169.0 6.0 %copy.73 = f32[320,3,3,320]{3,0,2,1:T(8,128)} copy(f32[320,3,3,320]{0,3,2,1:T(8,128)} %bitcast.184) | data formatting | bytes 7372800 | tf_op jit(solution)/shard_map/mul | solution.py:118
  175.0 1.7 fusion.82
  176.7 1.7 fusion.89
  178.4 1.7 fusion.92
  180.1 1.7 fusion.97
  181.9 3.2 fusion.20
  185.1 258.8 %all-reduce.12.cloned.1.call-done = f32[320,3,3,320]{3,0,2,1:T(8,128)} async-done(((f32[320,3,3,320]{3,0,2,1:T(8,128)}), f32[320,3,3,320]{3,0,2,1:T(8,128)}) %all-reduce.12.cloned.1.call-update) | async-done | bytes 3686416 | tf_op jit(solution)/shard_map/psum | solution.py:117
  444.0 1.9 constant_dynamic-slice_fusion
  (79 shorter events, 2.9 us)
Async XLA Ops:
  7.2 57.4 %copy-start = (bf16[1280,1280]{1,0:T(8,128)(2,1)S(1)}, bf16[1280,1280]{1,0:T(8,128)(2,1)}, u32[]{:S(2)}) copy-start(bf16[1280,1280]{1,0:T(8,128)(2,1)} %param.17) | copy-start | bytes 9830404
  7.2 436.8 %all-reduce.12.cloned.1.call-start = ((), (), s32[]{:S(2)}) async-start(), calls=%async_computation | async-start | bytes 8847360 | tf_op jit(solution)/shard_map/psum | solution.py:117
  8.1 61.8 %collective-permute-start.4 = (bf16[2,1,8,320]{3,2,1,0:T(8,128)(2,1)S(1)}, bf16[2,1,8,320]{3,2,1,0:T(8,128)(2,1)S(1)}, u32[]{:S(2)}, u32[]{:S(2)}) collective-permute-start(bf16[2,1,8,320]{3,2,1,0:T(8,128)(2,1)S(1)} %get-tuple-element.53), channel_id=1, source_target_pairs={{0,32},{32,64},{64,96},{96,128},{128,160},{160,192},{192,224},{1,3... | collective-permute-start | bytes 30728 | tf_op jit(solution)/shard_map/ppermute | solution.py:30
  12.6 57.5 %collective-permute-start.5 = (bf16[2,1,8,320]{3,2,1,0:T(8,128)(2,1)S(1)}, bf16[2,1,8,320]{3,2,1,0:T(8,128)(2,1)S(1)}, u32[]{:S(2)}, u32[]{:S(2)}) collective-permute-start(bf16[2,1,8,320]{3,2,1,0:T(8,128)(2,1)S(1)} %get-tuple-element.52), channel_id=1, source_target_pairs={{32,0},{64,32},{96,64},{128,96},{160,128},{192,160},{224,192},{33,... | collective-permute-start | bytes 30728 | tf_op jit(solution)/shard_map/ppermute | solution.py:31
  13.9 4.8 %copy-start.19 = (s32[2]{0:T(128)S(1)}, s32[2]{0:T(128)}, u32[]{:S(2)}) copy-start(s32[2]{0:T(128)} %param.11) | copy-start | bytes 28
  66.5 3.4 copy-start.6
  68.0 6.7 %copy-start.12 = (bf16[3,3,320,320]{3,2,1,0:T(8,128)(2,1)S(1)}, bf16[3,3,320,320]{3,2,1,0:T(8,128)(2,1)}, u32[]{:S(2)}) copy-start(bf16[3,3,320,320]{3,2,1,0:T(8,128)(2,1)} %param.14) | copy-start | bytes 5529604
  70.4 13.1 %collective-permute-start.7 = (bf16[2,66,1,320]{3,2,1,0:T(2,128)(2,1)S(1)}, bf16[2,66,1,320]{3,2,1,0:T(2,128)(2,1)S(1)}, u32[]{:S(2)}, u32[]{:S(2)}) collective-permute-start(bf16[2,66,1,320]{3,2,1,0:T(2,128)(2,1)S(1)} %get-tuple-element.42), channel_id=1, source_target_pairs={{0,1},{1,2},{2,3},{3,4},{4,5},{5,6},{6,7},{7,8},{8,9},{9,10},{10,1... | collective-permute-start | bytes 253448 | tf_op jit(solution)/shard_map/ppermute | solution.py:30
  72.5 9.7 %collective-permute-start.6 = (bf16[2,66,1,320]{3,2,1,0:T(2,128)(2,1)S(1)}, bf16[2,66,1,320]{3,2,1,0:T(2,128)(2,1)S(1)}, u32[]{:S(2)}, u32[]{:S(2)}) collective-permute-start(bf16[2,66,1,320]{3,2,1,0:T(2,128)(2,1)S(1)} %get-tuple-element.43), channel_id=1, source_target_pairs={{1,0},{2,1},{3,2},{4,3},{5,4},{6,5},{7,6},{8,7},{9,8},{10,9},{11,1... | collective-permute-start | bytes 253448 | tf_op jit(solution)/shard_map/ppermute | solution.py:31
  84.9 1.8 copy-start.8
  84.9 1.8 copy-start.15
  84.9 1.8 copy-start.17
  84.9 1.8 copy-start.18
  129.5 24.6 %copy-start.4 = (bf16[2,64,8,320]{3,2,1,0:T(8,128)(2,1)}, bf16[2,64,8,320]{3,2,1,0:T(8,128)(2,1)S(1)}, u32[]{:S(2)}) copy-start(bf16[2,64,8,320]{3,2,1,0:T(8,128)(2,1)S(1)} %get-tuple-element.49) | copy-start | bytes 1966084
  134.0 7.0 %collective-permute-start.1 = (bf16[2,1,8,320]{3,2,1,0:T(8,128)(2,1)S(1)}, bf16[2,1,8,320]{3,2,1,0:T(8,128)(2,1)S(1)}, u32[]{:S(2)}, u32[]{:S(2)}) collective-permute-start(bf16[2,1,8,320]{3,2,1,0:T(8,128)(2,1)S(1)} %get-tuple-element.55), channel_id=1, source_target_pairs={{32,0},{64,32},{96,64},{128,96},{160,128},{192,160},{224,192},{33,... | collective-permute-start | bytes 30728 | tf_op jit(solution)/shard_map/ppermute | solution.py:31
  135.3 5.7 %collective-permute-start = (bf16[2,1,8,320]{3,2,1,0:T(8,128)(2,1)S(1)}, bf16[2,1,8,320]{3,2,1,0:T(8,128)(2,1)S(1)}, u32[]{:S(2)}, u32[]{:S(2)}) collective-permute-start(bf16[2,1,8,320]{3,2,1,0:T(8,128)(2,1)S(1)} %get-tuple-element.54), channel_id=1, source_target_pairs={{0,32},{32,64},{64,96},{96,128},{128,160},{160,192},{192,224},{1,3... | collective-permute-start | bytes 30728 | tf_op jit(solution)/shard_map/ppermute | solution.py:30
  141.4 12.8 %collective-permute-start.3 = (bf16[2,66,1,320]{3,2,1,0:T(2,128)(2,1)S(1)}, bf16[2,66,1,320]{3,2,1,0:T(2,128)(2,1)S(1)}, u32[]{:S(2)}, u32[]{:S(2)}) collective-permute-start(bf16[2,66,1,320]{3,2,1,0:T(2,128)(2,1)S(1)} %get-tuple-element.46), channel_id=1, source_target_pairs={{1,0},{2,1},{3,2},{4,3},{5,4},{6,5},{7,6},{8,7},{9,8},{10,9},{11,1... | collective-permute-start | bytes 253448 | tf_op jit(solution)/shard_map/ppermute | solution.py:31
  144.2 10.0 %collective-permute-start.2 = (bf16[2,66,1,320]{3,2,1,0:T(2,128)(2,1)S(1)}, bf16[2,66,1,320]{3,2,1,0:T(2,128)(2,1)S(1)}, u32[]{:S(2)}, u32[]{:S(2)}) collective-permute-start(bf16[2,66,1,320]{3,2,1,0:T(2,128)(2,1)S(1)} %get-tuple-element.47), channel_id=1, source_target_pairs={{0,1},{1,2},{2,3},{3,4},{4,5},{5,6},{6,7},{7,8},{8,9},{9,10},{10,1... | collective-permute-start | bytes 253448 | tf_op jit(solution)/shard_map/ppermute | solution.py:30
  156.6 21.8 %copy-start.2 = (bf16[2,66,9,320]{3,2,1,0:T(8,128)(2,1)}, bf16[2,66,9,320]{3,2,1,0:T(8,128)(2,1)S(1)}, u32[]{:S(2)}) copy-start(bf16[2,66,9,320]{3,2,1,0:T(8,128)(2,1)S(1)} %get-tuple-element.44) | copy-start | bytes 2280964
  159.7 1.1 copy-start.7
  162.7 1.1 copy-start.5
  175.0 6.9 %copy-start.14 = (f32[2,64,8,320]{3,2,1,0:T(8,128)S(1)}, f32[2,64,8,320]{3,2,1,0:T(8,128)}, u32[]{:S(2)}) copy-start(f32[2,64,8,320]{3,2,1,0:T(8,128)} %fusion.30) | copy-start | bytes 3932164
  176.7 5.2 %copy-start.11 = (f32[2,64,8,320]{3,2,1,0:T(8,128)S(1)}, f32[2,64,8,320]{3,2,1,0:T(8,128)}, u32[]{:S(2)}) copy-start(f32[2,64,8,320]{3,2,1,0:T(8,128)} %fusion.79) | copy-start | bytes 3932164
  176.7 5.2 %copy-start.13 = (f32[2,64,8,320]{3,2,1,0:T(8,128)S(1)}, f32[2,64,8,320]{3,2,1,0:T(8,128)}, u32[]{:S(2)}) copy-start(f32[2,64,8,320]{3,2,1,0:T(8,128)} %fusion.34) | copy-start | bytes 3932164
  178.4 3.5 copy-start.10
  180.1 1.8 copy-start.3
  180.1 1.8 copy-start.9
  180.1 1.8 copy-start.16
  181.9 263.9 %copy-start.1 = (bf16[1280,1280]{1,0:T(8,128)(2,1)S(1)}, bf16[1280,1280]{1,0:T(8,128)(2,1)}, u32[]{:S(2)}) copy-start(bf16[1280,1280]{1,0:T(8,128)(2,1)} %param.17) | copy-start | bytes 9830404
Sparse Core Ops, SparseCore 0:
  175.1 268.8 all-reduce.11
where the time goes:
time: 455 us; the launch traced here: 453 us
  waiting for transfers between devices  265 us (58%)
  blocking collectives  80.2 us (18%)
  matrix products  44 us (10%)
  starting transfers between devices  22.6 us (5%)
  between operations  14.7 us (3%)
  other arithmetic  13.9 us (3%)
  local copies, waits for them, and re-layouts  12.4 us (3%)
    psum x1, waiting for transfers between devices, local(): lax.psum(jnp.stack(pieces, axis=1).reshape(channel_count, 3, 3, channel_c...  259 us
    psum x10, blocking collectives, one_axis_at_a_time(): return functools.reduce(lax.psum, axes, shard)  80.2 us
    dot_general x9, matrix products, local(): jnp.einsum('bhwc,cd->bhwd', padded[:, kh:kh + row_count, kw:kw + column_c...  21.5 us
    ppermute x4, starting transfers between devices, with_halo(): before = lax.ppermute(last, axis, up)  14.9 us
    dot_general x9, matrix products, local(): jnp.einsum('bhwd,cd->bhwc', gpad[:, 2 - kh:2 - kh + row_count, 2 - kw:2 -...  12.6 us
  transfers between devices with their start and end apart: 9, of which 2 were waited for; matrix products, arithmetic and copies ran while one was open for 7% of the time, Pallas kernels for 0%

commit v1 on v0

v1 whole, which is shorter than its diff:
```python
import functools
import math

import jax
import jax.numpy as jnp
from jax import lax
from jax.experimental import pallas as pl
from jax.experimental.pallas import tpu as pltpu
from jax.sharding import Mesh
from jax.sharding import PartitionSpec as P

AXES = ("row_0", "row_1", "col_0", "col_1", "col_2")
ROW = ("row_0", "row_1")
COL = ("col_0", "col_1", "col_2")
EPS = 1e-05
GROUP = 10
C, CP = 320, 384
TE = 1280
B = 2
W = 8
TOP, OWN, PADROWS = 7, 8, 80
KP = 1024
f32, bf16 = jnp.float32, jnp.bfloat16
MESH = pl.DeviceIdType.MESH


def widen(v):
    return jnp.concatenate([v, jnp.zeros(v.shape[:-1] + (CP - C,), v.dtype)], axis=-1)


def dot(a, b):
    return jnp.dot(a, b, preferred_element_type=f32)


def dot_nt(a, b):
    return lax.dot_general(a, b, (((1,), (1,)), ((), ())), preferred_element_type=f32)


def pack_taps(put, v0, v1, v2):
    r = pltpu.roll(v1, 64, 1)
    put(0, 256, v0[:, 0:256])
    put(256, 128, v0[:, 256:384] + r[:, 0:128])
    put(384, 256, r[:, 128:384])
    put(640, 384, v2)


def group_sums(v):
    i = lax.broadcasted_iota(jnp.int32, (CP, CP), 0)
    j = lax.broadcasted_iota(jnp.int32, (CP, CP), 1)
    same = ((i * 6554) >> 16) == ((j * 6554) >> 16)
    ones = jnp.where(same & (i < C) & (j < C), 1.0, 0.0).astype(bf16)
    hi = v.astype(bf16)
    rest = v - hi.astype(f32)
    mid = rest.astype(bf16)
    low = (rest - mid.astype(f32)).astype(bf16)
    return dot(hi, ones) + dot(mid, ones) + dot(low, ones)


def kernel(
    sizes,
    H,
    ts_ref, gain_ref, bias_ref, cb_ref, lat_hbm, cot_hbm, cw_hbm, ein_hbm, eout_hbm, tw_hbm,
    bo_hbm, ig_hbm, cwg_ref, st_ref, gs_ref, emb_ref,
    in_v, cw_v, ein_v, eout_v, tw_v,
    row_in, col_out, col_in, cor_out, cor_in,
    lt, t80, gx, xx, wf, wt, da, co_v, gt, wg,
    sb1, r1, sb2, r2, sb3, r3, agb,
    a1, b1, a2, b2, ob, og,
    ld_sem, st_sem, halo_s, halo_r, ar_s, ar_r, s1_s, s1_r, s2_s, s2_r, s3_s, s3_r, ag_s, ag_r,
):
    Y, ZL, X, ZH, CO = sizes
    y, zl, x, zh, co = (lax.axis_index(a) for a in AXES)
    row, col = y * ZL + zl, (x * ZH + zh) * CO + co
    NR, NC = Y * ZL, X * ZH * CO
    NA, NB, NP, NZ = ZH * ZL * CO, X * Y, CO * X, ZH * ZL
    PL = 3 * KP // NP
    RB = 40 // NR
    RBZ = ZL * RB
    count = float(GROUP * H * NR * W * NC)
    scale = 1.0 / math.sqrt(B * H * NR * W * NC)

    def dev(y_=None, zl_=None, x_=None, zh_=None, co_=None):
        return {
            "row_0": y if y_ is None else y_,
            "row_1": zl if zl_ is None else zl_,
            "col_0": x if x_ is None else x_,
            "col_1": zh if zh_ is None else zh_,
            "col_2": co if co_ is None else co_,
        }

    def dev_at(r, c):
        return dev(r // ZL, lax.rem(r, ZL), c // (ZH * CO), lax.rem(c // CO, ZH), lax.rem(c, CO))

    ia, ib, iz, ip = (zh * ZL + zl) * CO + co, x * Y + y, zh * ZL + zl, co * X + x

    def peer_a(k):
        j = lax.rem(ia + k, NA)
        return j, dev(zl_=lax.rem(j // CO, ZL), zh_=j // (CO * ZL), co_=lax.rem(j, CO))

    def peer_b(k):
        j = lax.rem(ib + k, NB)
        return j, dev(x_=j // Y, y_=lax.rem(j, Y))

    def peer_z(k):
        j = lax.rem(iz + k, NZ)
        return j, dev(zl_=lax.rem(j, ZL), zh_=j // ZL)

    def peer_p(k):
        j = lax.rem(ip + k, NP)
        return j, dev(co_=j // X, x_=lax.rem(j, X))

    up, down = lax.rem(row + NR - 1, NR), lax.rem(row + 1, NR)
    left, right = lax.rem(col + NC - 1, NC), lax.rem(col + 1, NC)
    near = [dev_at(r, c) for r in (up, row, down) for c in (left, col, right) if not (r is row and c is col)]

    loads = [
        pltpu.make_async_copy(s, d, ld_sem.at[i])
        for i, (s, d) in enumerate(
            ((lat_hbm, in_v.at[0]), (cot_hbm, in_v.at[1]), (cw_hbm, cw_v), (ein_hbm, ein_v), (eout_hbm, eout_v), (tw_hbm, tw_v))
        )
    ]
    for cp in loads:
        cp.start()
    barrier = pltpu.get_barrier_semaphore()
    greeted = (
        [peer_a(k)[1] for k in range(1, NA)]
        + [peer_b(k)[1] for k in range(1, NB)]
        + [peer_p(k)[1] for k in range(1, NP)]
        + near
    )
    for d in greeted:
        pl.semaphore_signal(barrier, inc=1, device_id=d, device_id_type=MESH)

    sends = []

    def send(src, dst, s, r, d):
        cp = pltpu.make_async_remote_copy(src_ref=src, dst_ref=dst, send_sem=s, recv_sem=r, device_id=d, device_id_type=MESH)
        cp.start()
        sends.append(cp)
        return cp

    def zero(i, _):
        lt[i // (B * 10), lax.rem(i // 10, B), lax.rem(i, 10)] = jnp.zeros((PADROWS, CP), f32)
        return 0

    lax.fori_loop(0, 2 * B * 10, zero, 0)
    t80[...] = jnp.zeros_like(t80)

    def turn(arr, b, squares):
        def body(i, carry):
            h = pl.multiple_of(i * 8, 8)
            v = in_v[arr, b, pl.ds(h, 8)].astype(f32)
            lt[arr, b, 1:9, pl.ds(h + OWN, 8), 0:C] = jnp.transpose(v, (1, 0, 2))
            s = carry[0] + jnp.sum(v, axis=0)
            return (s, carry[1] + jnp.sum(v * v, axis=0)) if squares else (s,)

        z = jnp.zeros((W, C), f32)
        out = lax.fori_loop(0, H // 8, body, (z, z) if squares else (z,))
        return [widen(jnp.sum(o, axis=0, keepdims=True)) for o in out]

    loads[0].wait()
    sums = [turn(0, b, True) for b in range(B)]
    a1[ia] = jnp.concatenate([sums[0][0], sums[1][0], sums[0][1], sums[1][1], jnp.zeros((4, CP), f32)], axis=0)

    pl.semaphore_wait(barrier, len(greeted))

    def exchange(buf, own, sem, peers, n):
        for k in range(1, n):
            send(buf.at[own], buf.at[own], ar_s.at[sem, k], ar_r.at[sem, own], peers(k)[1])

    def gather_sum(buf, own, sem, peers, n):
        for k in range(1, n):
            j, d = peers(k)
            pltpu.make_async_remote_copy(
                src_ref=buf.at[j], dst_ref=buf.at[j], send_sem=ar_s.at[sem, k], recv_sem=ar_r.at[sem, j], device_id=d, device_id_type=MESH
            ).wait_recv()
        total = buf[0]
        for j in range(1, n):
            total = total + buf[j]
        return total

    exchange(a1, ia, 0, peer_a, NA)

    halos = []

    def halo(src, dst, i, d):
        halos.append(send(src, dst, halo_s.at[i], halo_r.at[i], d))

    loads[1].wait()
    for arr in range(2):
        halo(in_v.at[arr, :, H - 1], row_in.at[0, arr], arr, dev_at(down, col))
        halo(in_v.at[arr, :, 0], row_in.at[1, arr], 2 + arr, dev_at(up, col))
    gsum = [turn(1, b, False)[0] for b in range(B)]
    for arr in range(2):
        for b in range(B):
            col_out[0, arr, b] = lt[arr, b, 1, OWN : OWN + H, 0:C].astype(bf16)
            col_out[1, arr, b] = lt[arr, b, W, OWN : OWN + H, 0:C].astype(bf16)
            for r in range(2):
                for c in range(2):
                    i = OWN + (H - 1) * r
                    k = arr * B + b
                    cor_out[2 * r + c, k : k + 1, :] = lt[arr, b, 1 + (W - 1) * c, i : i + 1, :]
    for arr in range(2):
        halo(col_out.at[1, arr], col_in.at[0, arr], 4 + arr, dev_at(row, right))
        halo(col_out.at[0, arr], col_in.at[1, arr], 6 + arr, dev_at(row, left))
    for r in range(2):
        for c in range(2):
            halo(cor_out.at[2 * r + c], cor_in.at[2 * (1 - r) + 1 - c], 8 + 2 * r + c, dev_at((up, down)[r], (left, right)[c]))

    loads[2].wait()
    for kw in range(3):
        for kh in range(3):
            wf[kw, kh * C : (kh + 1) * C, :] = cw_v[kh, kw]
        wf[kw, 3 * C : KP, :] = jnp.zeros((KP - 3 * C, C), bf16)

        def turn_w(i, _):
            n = pl.multiple_of(i * 64, 64)
            v = [widen(cw_v[2 - kh, 2 - kw, pl.ds(n, 64), :].astype(f32)) for kh in range(3)]

            def put(at, wide, value):
                wt[kw, pl.ds(n, 64), at : at + wide] = value.astype(bf16)

            pack_taps(put, *v)
            return 0

        lax.fori_loop(0, C // 64, turn_w, 0)

    for cp in loads[3:]:
        cp.wait()
    lane = lax.broadcasted_iota(jnp.int32, (8, C), 1)
    step = jnp.where(lane < C // 2, lane, lane - C // 2).astype(f32)
    which = lax.broadcasted_iota(jnp.int32, (8, C), 0)
    time = jnp.where(which == 0, ts_ref[0].astype(f32), ts_ref[1].astype(f32))
    angle = time * jnp.exp(-math.log(10000.0) * step / (C // 2))
    sinus = jnp.where(lane < C // 2, jnp.cos(angle), jnp.sin(angle)).astype(bf16)
    hidden = jax.nn.silu(dot(sinus, ein_v[...])).astype(bf16)
    emb = jax.nn.silu(dot(hidden, eout_v[...])).astype(bf16)
    emb_ref[...] = emb.astype(f32)
    temb = dot(emb, tw_v[...]) + cb_ref[...].reshape(1, C)

    b1[ib] = gather_sum(a1, ia, 0, peer_a, NA)
    exchange(b1, ib, 1, peer_b, NB)

    for cp in halos:
        cp.wait_recv()
    keep = [
        jnp.where(row > 0, 1.0, 0.0),
        jnp.where(row < NR - 1, 1.0, 0.0),
        jnp.where(col > 0, 1.0, 0.0),
        jnp.where(col < NC - 1, 1.0, 0.0),
    ]
    for arr in range(2):
        for b in range(B):
            for side in range(2):
                at = OWN + H if side else TOP
                v = row_in[side, arr, b].astype(f32) * keep[side]
                for w in range(W):
                    lt[arr, b, w + 1, at : at + 1, 0:C] = v[w : w + 1]
                lt[arr, b, 9 * side, OWN : OWN + H, 0:C] = col_in[side, arr, b].astype(f32) * keep[2 + side]
                for c in range(2):
                    k = arr * B + b
                    lt[arr, b, 9 * c, at : at + 1, :] = cor_in[2 * side + c, k : k + 1, :] * keep[side] * keep[2 + c]

    def build_g(i, _):
        b, wq = i // 10, lax.rem(i, 10)

        def put(at, wide, value):
            gx[b, wq, :, at : at + wide] = value.astype(bf16)

        pack_taps(put, *(lt[1, b, wq, TOP + k : TOP + k + H, :] for k in range(3)))
        return 0

    lax.fori_loop(0, B * 10, build_g, 0)

    def dacts(i, _):
        b, w = i // 2, lax.rem(i, 2) * 4
        acc = dot_nt(gx[b, pl.ds(w, 4)].reshape(4 * H, KP), wt[0])
        for kw in range(1, 3):
            acc = acc + dot_nt(gx[b, pl.ds(w + kw, 4)].reshape(4 * H, KP), wt[kw])
        da[b, pl.ds(w, 4)] = widen(acc).reshape(4, H, CP)
        return 0

    lax.fori_loop(0, 2 * B, dacts, 0)
    part = max(128 // H, 1)
    for b in range(B):
        for k in range(W // part):
            v = lt[1, b, 1 + k * part : 1 + (k + 1) * part, OWN : OWN + H, :].reshape(part * H, CP)
            gt[b, :, k * part * H : (k + 1) * part * H] = jnp.transpose(v).astype(bf16)

    means = group_sums(gather_sum(b1, ib, 1, peer_b, NB)) / count
    gain, bias = widen(gain_ref[...].reshape(1, C)), widen(bias_ref[...].reshape(1, C))
    mean = [means[b : b + 1] for b in range(B)]
    rstd = [lax.rsqrt(means[B + b : B + b + 1] - mean[b] * mean[b] + EPS) for b in range(B)]
    line = lax.broadcasted_iota(jnp.int32, (PADROWS, CP), 0)
    rows_kept = jnp.where(line < OWN, keep[0], jnp.where(line < OWN + H, 1.0, keep[1]))

    def activate(b, wq, side_kept):
        mul = rstd[b] * gain
        normed = lt[0, b, wq] * mul + (bias - mean[b] * mul)
        sig = jax.nn.sigmoid(normed)
        t80[...] = normed * sig * (rows_kept * side_kept)

        def put(at, wide, value):
            xx[b, wq, :, at : at + wide] = value.astype(bf16)

        pack_taps(put, *(t80[TOP + k : TOP + k + H, :] for k in range(3)))
        return normed, sig

    halves = []
    for b in range(B):

        def own_column(w, carry):
            normed, sig = activate(b, w + 1, 1.0)
            normed, sig = normed[OWN : OWN + H], sig[OWN : OWN + H]
            dn = da[b, w] * sig * (1.0 + normed * (1.0 - sig))
            da[b, w] = dn
            xhat = (lt[0, b, w + 1, OWN : OWN + H, :] - mean[b]) * rstd[b]
            return (
                carry[0] + jnp.sum(dn.reshape(H // 8, 8, CP), axis=0),
                carry[1] + jnp.sum((dn * xhat).reshape(H // 8, 8, CP), axis=0),
            )

        z = jnp.zeros((8, CP), f32)
        halves.append([jnp.sum(o, axis=0, keepdims=True) for o in lax.fori_loop(0, W, own_column, (z, z))])
    a2[ia] = jnp.concatenate(
        [halves[0][0], halves[1][0], halves[0][1], halves[1][1], gsum[0], gsum[1], jnp.zeros((2, CP), f32)], axis=0
    )
    exchange(a2, ia, 2, peer_a, NA)
    for b in range(B):
        activate(b, 0, keep[2])
        activate(b, 9, keep[3])

    per = PL // 128
    for kw in range(3):
        for n in range(4):
            r = dot(gt[0, 0:C], xx[0, kw : kw + W, :, n * 256 : (n + 1) * 256].reshape(W * H, 256))
            r = r + dot(gt[1, 0:C], xx[1, kw : kw + W, :, n * 256 : (n + 1) * 256].reshape(W * H, 256))
            for t in range(2):
                tile = kw * 8 + n * 2 + t
                at = tile % per * 128
                wg[tile // per, :, at : at + 128] = r[:, t * 128 : (t + 1) * 128]

    def to_partner(i, _):
        sb1[i] = wg[(1 - co) * X + i].reshape(40, 8, PL).astype(bf16)
        return 0

    lax.fori_loop(0, X, to_partner, 0)
    first = send(sb1, r1, s1_s.at[0], s1_r.at[0], dev(co_=1 - co))

    def conv(b):
        def body(i, _):
            w = i * 4
            acc = dot(xx[b, pl.ds(w, 4)].reshape(4 * H, KP), wf[0])
            for kw in range(1, 3):
                acc = acc + dot(xx[b, pl.ds(w + kw, 4)].reshape(4 * H, KP), wf[kw])
            co_v[b, pl.ds(w, 4), :, 0:C] = acc.reshape(4, H, C)
            return 0

        lax.fori_loop(0, 2, body, 0)

        def emit(i, _):
            h = pl.multiple_of(i * 8, 8)
            v = co_v[b, :, pl.ds(h, 8), 0:C] + lt[0, b, 1:9, pl.ds(h + OWN, 8), 0:C] + temb[b : b + 1]
            ob[b, pl.ds(h, 8)] = jnp.transpose(v, (1, 0, 2)).astype(bf16)
            return 0

        lax.fori_loop(0, H // 8, emit, 0)
        out = pltpu.make_async_copy(ob.at[b], bo_hbm.at[b], st_sem.at[b])
        out.start()
        return out

    stores = [conv(0)]
    first.wait_recv()

    def halve(i, _):
        v = wg[co * X + i] + r1[i].astype(f32).reshape(C, PL)
        wg[co * X + i] = v
        sb2[i] = v.reshape(40, 8, PL).astype(bf16)
        return 0

    lax.fori_loop(0, X, halve, 0)
    second = []
    for dx in range(X):
        for dy in range(Y):
            if dx or dy:
                px, py = lax.rem(x + dx, X), lax.rem(y + dy, Y)
                k = dx * Y + dy
                second.append(send(sb2.at[px, pl.ds(py * RBZ, RBZ)], r2.at[k], s2_s.at[k], s2_r.at[k], dev(x_=px, y_=py)))
    b2[ib] = gather_sum(a2, ia, 2, peer_a, NA)
    exchange(b2, ib, 3, peer_b, NB)
    stores.append(conv(1))

    totals = gather_sum(b2, ib, 3, peer_b, NB)
    weights = jnp.concatenate([totals[0:4] * gain, jnp.zeros((4, CP), f32)], axis=0)
    groups = group_sums(weights) / count
    for b in range(B):
        m1, m2 = groups[b : b + 1, 0:C], groups[B + b : B + b + 1, 0:C]
        mb, rb = mean[b][:, 0:C], rstd[b][:, 0:C]

        def emit(i, _):
            h = pl.multiple_of(i * 8, 8)
            xv = lt[0, b, 1:9, pl.ds(h + OWN, 8), 0:C]
            gv = lt[1, b, 1:9, pl.ds(h + OWN, 8), 0:C]
            dn = da[b, :, pl.ds(h, 8), 0:C]
            v = gv + rb * (dn * gain[:, 0:C] - m1 - (xv - mb) * rb * m2)
            og[b, pl.ds(h, 8)] = jnp.transpose(v, (1, 0, 2))
            return 0

        lax.fori_loop(0, H // 8, emit, 0)
        out = pltpu.make_async_copy(og.at[b], ig_hbm.at[b], st_sem.at[B + b])
        out.start()
        stores.append(out)
    st_ref[...] = jnp.concatenate(
        [totals[2:3] + totals[3:4], totals[0:1] + totals[1:2], totals[4:5] + totals[5:6], jnp.zeros((5, CP), f32)], axis=0
    )[:, 0:C] * scale
    gs_ref[...] = jnp.concatenate([totals[4:6], jnp.zeros((6, CP), f32)], axis=0)[:, 0:C]

    for cp in second:
        cp.wait_recv()
    mine = wg[co * X + x, pl.ds(pl.multiple_of(y * (RBZ * 8), 8), RBZ * 8), :].reshape(RBZ, 8, PL)
    for k in range(1, NB):
        mine = mine + r2[k].astype(f32)
    sb3[...] = mine.astype(bf16)
    for k in range(1, NZ):
        j, d = peer_z(k)
        send(sb3.at[pl.ds(lax.rem(j, ZL) * RB, RB)], r3.at[iz], s3_s.at[k], s3_r.at[iz], d)
    r3[iz] = sb3[pl.ds(zl * RB, RB)]
    for k in range(1, NZ):
        j, d = peer_z(k)
        pltpu.make_async_remote_copy(
            src_ref=r3.at[j], dst_ref=r3.at[j], send_sem=s3_s.at[k], recv_sem=s3_r.at[j], device_id=d, device_id_type=MESH
        ).wait_recv()
    total = r3[0].astype(f32)
    for j in range(1, NZ):
        total = total + r3[j].astype(f32)
    agb[ip] = total.astype(bf16)
    for k in range(1, NP):
        send(agb.at[ip], agb.at[ip], ag_s.at[k], ag_r.at[ip], peer_p(k)[1])
    for k in range(1, NP):
        j, d = peer_p(k)
        pltpu.make_async_remote_copy(
            src_ref=agb.at[j], dst_ref=agb.at[j], send_sem=ag_s.at[k], recv_sem=ag_r.at[j], device_id=d, device_id_type=MESH
        ).wait_recv()
    for p in range(NP):
        cwg_ref[:, p * PL : (p + 1) * PL] = agb[p].astype(f32).reshape(RB * 8, PL) * scale
    for cp in sends:
        cp.wait_send()
    for cp in stores:
        cp.wait()


def step(sizes, latent, timestep, gain, bias, conv_w, conv_b, embed_in, embed_out, time_w, cotangent):
    Y, ZL, X, ZH, CO = sizes
    H = latent.shape[1]
    NA, NB, NP, NZ = ZH * ZL * CO, X * Y, CO * X, ZH * ZL
    PL = 3 * KP // NP
    RB = 40 // (Y * ZL)
    anyspace = pl.BlockSpec(memory_space=pl.ANY)
    vmem = pl.BlockSpec(memory_space=pltpu.VMEM)
    V, D = pltpu.VMEM, pltpu.SemaphoreType.DMA
    NG = max(NA, NB)
    bo, ig, cwg, st, gs, emb = pl.pallas_call(
        functools.partial(kernel, sizes, H),
        out_shape=(
            jax.ShapeDtypeStruct((B, H, W, C), bf16),
            jax.ShapeDtypeStruct((B, H, W, C), f32),
            jax.ShapeDtypeStruct((RB * 8, 3 * KP), f32),
            jax.ShapeDtypeStruct((8, C), f32),
            jax.ShapeDtypeStruct((8, C), f32),
            jax.ShapeDtypeStruct((8, TE), f32),
        ),
        in_specs=[pl.BlockSpec(memory_space=pltpu.SMEM)] + [vmem] * 3 + [anyspace] * 6,
        out_specs=(anyspace, anyspace, vmem, vmem, vmem, vmem),
        scratch_shapes=[
            V((2, B, H, W, C), bf16),
            V((3, 3, C, C), bf16),
            V((C, TE), bf16),
            V((TE, TE), bf16),
            V((TE, C), bf16),
            V((2, 2, B, W, C), bf16),
            V((2, 2, B, H, C), bf16),
            V((2, 2, B, H, C), bf16),
            V((4, 8, CP), f32),
            V((4, 8, CP), f32),
            V((2, B, 10, PADROWS, CP), f32),
            V((PADROWS, CP), f32),
            V((B, 10, H, KP), bf16),
            V((B, 10, H, KP), bf16),
            V((3, KP, C), bf16),
            V((3, C, KP), bf16),
            V((B, W, H, CP), f32),
            V((B, W, H, CP), f32),
            V((B, CP, W * H), bf16),
            V((NP, C, PL), f32),
            V((X, 40, 8, PL), bf16),
            V((X, 40, 8, PL), bf16),
            V((X, 40, 8, PL), bf16),
            V((NB, ZL * RB, 8, PL), bf16),
            V((ZL * RB, 8, PL), bf16),
            V((NZ, RB, 8, PL), bf16),
            V((NP, RB, 8, PL), bf16),
            V((NA, 8, CP), f32),
            V((NB, 8, CP), f32),
            V((NA, 8, CP), f32),
            V((NB, 8, CP), f32),
            V((B, H, W, C), bf16),
            V((B, H, W, C), f32),
            D((6,)),
            D((2 * B,)),
            D((12,)),
            D((12,)),
            D((4, NG)),
            D((4, NG)),
            D((1,)),
            D((1,)),
            D((NB,)),
            D((NB,)),
            D((NZ,)),
            D((NZ,)),
            D((NP,)),
            D((NP,)),
        ],
        compiler_params=pltpu.CompilerParams(collective_id=0, has_side_effects=True, vmem_limit_bytes=62 * 1024 * 1024),
        name="block",
    )(timestep, gain, bias, conv_b, latent, cotangent, conv_w, embed_in, embed_out, time_w)
    scale = 1.0 / math.sqrt(B * H * Y * ZL * W * X * ZH * CO)
    conv_w_grad = cwg.reshape(RB * 8, 3, KP)[:, :, : 3 * C].reshape(RB * 8, 3, 3, C).transpose(0, 2, 1, 3)
    time_w_grad = lax.dot_general(emb[0:B], gs[0:B], (((0,), (0,)), ((), ()))) * scale
    return bo, ig, conv_w_grad, st[0], st[1], st[2], time_w_grad


def build(finer):
    sizes = tuple(finer.shape[a] for a in AXES)
    image = P(None, ROW, COL, None)
    return jax.shard_map(
        functools.partial(step, sizes),
        mesh=finer,
        in_specs=(image, P(), P(), P(), P(), P(), P(), P(), P(), image),
        out_specs=(image, image, P(ROW, None, None, None), P(), P(), P(), P()),
        check_vma=False,
    )


def solution(mesh):
    return build(Mesh(mesh.devices.reshape(4, 2, 4, 4, 2), AXES))
```

time: 455 us -> 85.4 us (0.19)
  waiting for transfers between devices: 265 us -> 0 us
  blocking collectives: 80.2 us -> 0 us
  Pallas kernels: 0 us -> 74.4 us
  matrix products: 44 us -> 1.59 us
  starting transfers between devices: 22.6 us -> 0 us
  between operations: 14.7 us -> 0.69 us
  other arithmetic: 13.9 us -> 0 us
    psum x1 -> x0, waiting for transfers between devices: 259 us -> none  [local(): lax.psum(jnp.stack(pieces, axis=1).reshape(channel_count, 3, 3, channel_c...]
    psum x10 -> x0, blocking collectives: 80.2 us -> none  [one_axis_at_a_time(): return functools.reduce(lax.psum, axes, shard)]
    pallas_call x0 -> x1, Pallas kernels: none -> 74.4 us  [step(): pl.pallas_call(functools.partial(kernel, sizes, H), out_shape=(jax.ShapeD...]
    dot_general x30 -> x1, matrix products: 44 us -> 1.59 us  [step(): lax.dot_general(emb[0:B], gs[0:B], (((0,), (0,)), ((), ()))) * scale]
    ppermute x8 -> x0, starting transfers between devices: 22.5 us -> none  [the longest x4 14.9 us: with_halo(): before = lax.ppermute(last, axis, up)]
    mul x5 -> x0, local copies, waits for them, and re-layouts: 6.35 us -> none  [the longest x1 5.97 us: local(): jnp.stack(pieces, axis=1).reshape(channel_count, 3, 3, channel_count)]
    ppermute x8 -> x0, waiting for transfers between devices: 6.15 us -> none  [the longest x4 6.14 us: with_halo(): after = lax.ppermute(first, axis, down)]
  transfers between devices with their start and end apart: 9 -> 0, of which waited for: 2 -> 0; matrix products, arithmetic and copies ran while one was open for 7% -> 0% of each run, Pallas kernels for 0% -> 0%
where the time goes in v1:
time: 85.4 us; the launch traced here: 85.1 us
  Pallas kernels  74.4 us (87%)
  local copies, waits for them, and re-layouts  8.47 us (10%)
  matrix products  1.59 us (2%)
    pallas_call x1, Pallas kernels, step(): pl.pallas_call(functools.partial(kernel, sizes, H), out_shape=(jax.ShapeD...  74.4 us
    unnamed x12, local copies, waits for them, and re-layouts  5.09 us

profile of v1, /device:TPU:1, one launch (start us, length us, event | category | flops | bytes accessed | tf_op | source)
XLA Modules:
  0.0 85.1 jit_solution(3656762911467163008)
XLA Ops:
  0.6 2.2 %copy.18.tw_hbm = bf16[1280,320]{1,0:T(8,128)(2,1)} copy(bf16[1280,320]{0,1:T(8,128)(2,1)} %param.18) | data formatting | bytes 1638400 | tf_op args[8]
  2.8 74.4 %block.1 = (bf16[2,64,8,320]{3,2,1,0:T(8,128)(2,1)}, f32[2,64,8,320]{3,2,1,0:T(8,128)}, f32[40,3072]{1,0:T(8,128)}, f32[8,320]{1,0:T(8,128)}, f32[8,320]{1,0:T(8,128)}, /*index=5*/f32[8,1280]{1,0:T(8,128)}) custom-call(s32[2]{0:T(128)} %ts_ref.1, f32[320]{0:T(512)} %gain_ref.1, f32[320]{0:T(512)} %bias_ref.1, f32[320]{0:T(512)} %cb_ref.1, ...), custom_call_target="tpu_custom_call" | custom-call | tf_op jit(solution)/shard_map/block/pallas_call | solution.py:462
  77.2 1.4 %slice_reduce_fusion = (f32[320]{0:T(512)}, f32[320]{0:T(512)}, f32[320]{0:T(512)}) fusion(f32[8,320]{1,0:T(8,128)} %get-tuple-element.16), kind=kLoop, calls=%fused_computation.3 | loop fusion | bytes 7680 | tf_op jit(solution)/shard_map/slice | solution.py:529
  78.7 1.4 %reshape.20 = f32[40,3,1024]{2,1,0:T(4,128)S(1)} reshape(f32[40,3072]{1,0:T(8,128)} %get-tuple-element.15) | data formatting | bytes 983040 | tf_op jit(solution)/shard_map/reshape | solution.py:527
  80.1 0.0 copy-start.2
  80.1 0.0 copy-start.3
  80.1 0.3 copy.19
  80.4 0.3 reshape.21
  80.7 0.0 copy-start.1
  80.7 0.8 copy.20
  81.5 0.0 copy-done.2
  81.5 0.0 copy-done.3
  81.5 0.0 copy-start
  81.5 1.6 %convolution_multiply_fusion = f32[1280,320]{0,1:T(8,128)} fusion(f32[8,1280]{1,0:T(8,128)S(1)} %copy-done.2, f32[8,320]{1,0:T(8,128)S(1)} %copy-done.3), kind=kOutput, calls=%fused_computation | convolution fusion | flops 2048000 | bytes 1645056 | tf_op jit(solution)/shard_map/dot_general | solution.py:528
  83.1 0.0 copy-done.1
  83.1 0.9 %copy.23 = bf16[2,64,8,320]{3,2,1,0:T(8,128)(2,1)} copy(bf16[2,64,8,320]{3,2,1,0:T(8,128)(2,1)S(1)} %copy-done.1) | data formatting | bytes 1310720
  84.0 0.0 copy-done
  84.0 1.1 %copy.24 = f32[2,64,8,320]{3,2,1,0:T(8,128)} copy(f32[2,64,8,320]{3,2,1,0:T(8,128)S(1)} %copy-done) | data formatting | bytes 2621440
Async XLA Ops:
  80.1 1.5 %copy-start.2 = (f32[8,1280]{1,0:T(8,128)S(1)}, f32[8,1280]{1,0:T(8,128)}, u32[]{:S(2)}) copy-start(f32[8,1280]{1,0:T(8,128)} %get-tuple-element.17) | copy-start | bytes 122884
  80.1 1.5 %copy-start.3 = (f32[8,320]{1,0:T(8,128)S(1)}, f32[8,320]{1,0:T(8,128)}, u32[]{:S(2)}) copy-start(f32[8,320]{1,0:T(8,128)} %get-tuple-element.18) | copy-start | bytes 30724
  80.7 2.4 %copy-start.1 = (bf16[2,64,8,320]{3,2,1,0:T(8,128)(2,1)S(1)}, bf16[2,64,8,320]{3,2,1,0:T(8,128)(2,1)}, u32[]{:S(2)}) copy-start(bf16[2,64,8,320]{3,2,1,0:T(8,128)(2,1)} %get-tuple-element.36) | copy-start | bytes 1966084
  81.5 2.5 %copy-start = (f32[2,64,8,320]{3,2,1,0:T(8,128)S(1)}, f32[2,64,8,320]{3,2,1,0:T(8,128)}, u32[]{:S(2)}) copy-start(f32[2,64,8,320]{3,2,1,0:T(8,128)} %get-tuple-element.37) | copy-start | bytes 3932164

commit v2 on v1

--- a/solution.py
+++ b/solution.py
@@ -44,16 +44,36 @@
     put(640, 384, v2)
 
 
-def group_sums(v):
-    i = lax.broadcasted_iota(jnp.int32, (CP, CP), 0)
-    j = lax.broadcasted_iota(jnp.int32, (CP, CP), 1)
-    same = ((i * 6554) >> 16) == ((j * 6554) >> 16)
-    ones = jnp.where(same & (i < C) & (j < C), 1.0, 0.0).astype(bf16)
+def dot_exact(v, ones):
     hi = v.astype(bf16)
     rest = v - hi.astype(f32)
     mid = rest.astype(bf16)
     low = (rest - mid.astype(f32)).astype(bf16)
     return dot(hi, ones) + dot(mid, ones) + dot(low, ones)
+
+
+def own_lanes():
+    r = lax.broadcasted_iota(jnp.int32, (8, 128), 0)
+    lane = lax.broadcasted_iota(jnp.int32, (8, 128), 1)
+    return (lane >> 5) == r
+
+
+def pack_groups(v):
+    c = lax.broadcasted_iota(jnp.int32, (CP, 128), 0)
+    lane = lax.broadcasted_iota(jnp.int32, (CP, 128), 1)
+    ones = jnp.where((((c * 6554) >> 16) == (lane & 31)) & (c < C), 1.0, 0.0).astype(bf16)
+    return jnp.sum(jnp.where(own_lanes(), dot_exact(v, ones), 0.0), axis=0, keepdims=True)
+
+
+def spread_groups(t):
+    lane = lax.broadcasted_iota(jnp.int32, (128, CP), 0)
+    c = lax.broadcasted_iota(jnp.int32, (128, CP), 1)
+    ones = jnp.where((((c * 6554) >> 16) == (lane & 31)) & (c < C), 1.0, 0.0).astype(bf16)
+    return dot_exact(jnp.where(own_lanes(), jnp.broadcast_to(t, (8, 128)), 0.0), ones)
+
+
+def stacked(rows, n):
+    return jnp.concatenate(rows + [jnp.zeros((n - len(rows), CP), f32)], axis=0) if len(rows) < n else jnp.concatenate(rows, axis=0)
 
 
 def kernel(
@@ -64,8 +84,8 @@
     in_v, cw_v, ein_v, eout_v, tw_v,
     row_in, col_out, col_in, cor_out, cor_in,
     lt, t80, gx, xx, wf, wt, da, co_v, gt, wg,
-    sb1, r1, sb2, r2, sb3, r3, agb,
-    a1, b1, a2, b2, ob, og,
+    sb1, r1, sb2, r2, sb3, r3, agb, wide, slope,
+    a1, b1, a2, b2, a3, b3, ob, og,
     ld_sem, st_sem, halo_s, halo_r, ar_s, ar_r, s1_s, s1_r, s2_s, s2_r, s3_s, s3_r, ag_s, ag_r,
 ):
     Y, ZL, X, ZH, CO = sizes
@@ -160,7 +180,7 @@
 
     loads[0].wait()
     sums = [turn(0, b, True) for b in range(B)]
-    a1[ia] = jnp.concatenate([sums[0][0], sums[1][0], sums[0][1], sums[1][1], jnp.zeros((4, CP), f32)], axis=0)
+    a1[ia] = pack_groups(stacked([sums[0][0], sums[1][0], sums[0][1], sums[1][1]], 8))
 
     pl.semaphore_wait(barrier, len(greeted))
 
@@ -224,6 +244,14 @@
             return 0
 
         lax.fori_loop(0, C // 64, turn_w, 0)
+    part = max(128 // H, 1)
+    for b in range(B):
+        for k in range(W // part):
+            v = lt[1, b, 1 + k * part : 1 + (k + 1) * part, OWN : OWN + H, :].reshape(part * H, CP)
+            gt[b, :, k * part * H : (k + 1) * part * H] = jnp.transpose(v).astype(bf16)
+
+    b1[ib] = gather_sum(a1, ia, 0, peer_a, NA)
+    exchange(b1, ib, 1, peer_b, NB)
 
     for cp in loads[3:]:
         cp.wait()
@@ -236,10 +264,7 @@
     hidden = jax.nn.silu(dot(sinus, ein_v[...])).astype(bf16)
     emb = jax.nn.silu(dot(hidden, eout_v[...])).astype(bf16)
     emb_ref[...] = emb.astype(f32)
-    temb = dot(emb, tw_v[...]) + cb_ref[...].reshape(1, C)
-
-    b1[ib] = gather_sum(a1, ia, 0, peer_a, NA)
-    exchange(b1, ib, 1, peer_b, NB)
+    temb = dot_nt(emb, tw_v[...]) + cb_ref[...].reshape(1, C)
 
     for cp in halos:
         cp.wait_recv()
@@ -262,73 +287,50 @@
                     lt[arr, b, 9 * c, at : at + 1, :] = cor_in[2 * side + c, k : k + 1, :] * keep[side] * keep[2 + c]
 
     def build_g(i, _):
-        b, wq = i // 10, lax.rem(i, 10)
-
-        def put(at, wide, value):
-            gx[b, wq, :, at : at + wide] = value.astype(bf16)
-
-        pack_taps(put, *(lt[1, b, wq, TOP + k : TOP + k + H, :] for k in range(3)))
+        for b in range(B):
+            for n in range(2):
+                wq = i * 2 + n
+
+                def put(at, wide, value):
+                    gx[b, wq, :, at : at + wide] = value.astype(bf16)
+
+                pack_taps(put, *(lt[1, b, wq, TOP + k : TOP + k + H, :] for k in range(3)))
         return 0
 
-    lax.fori_loop(0, B * 10, build_g, 0)
-
-    def dacts(i, _):
-        b, w = i // 2, lax.rem(i, 2) * 4
-        acc = dot_nt(gx[b, pl.ds(w, 4)].reshape(4 * H, KP), wt[0])
-        for kw in range(1, 3):
-            acc = acc + dot_nt(gx[b, pl.ds(w + kw, 4)].reshape(4 * H, KP), wt[kw])
-        da[b, pl.ds(w, 4)] = widen(acc).reshape(4, H, CP)
-        return 0
-
-    lax.fori_loop(0, 2 * B, dacts, 0)
-    part = max(128 // H, 1)
-    for b in range(B):
-        for k in range(W // part):
-            v = lt[1, b, 1 + k * part : 1 + (k + 1) * part, OWN : OWN + H, :].reshape(part * H, CP)
-            gt[b, :, k * part * H : (k + 1) * part * H] = jnp.transpose(v).astype(bf16)
-
-    means = group_sums(gather_sum(b1, ib, 1, peer_b, NB)) / count
+    lax.fori_loop(0, 5, build_g, 0)
+
+    means = spread_groups(gather_sum(b1, ib, 1, peer_b, NB)) / count
     gain, bias = widen(gain_ref[...].reshape(1, C)), widen(bias_ref[...].reshape(1, C))
     mean = [means[b : b + 1] for b in range(B)]
     rstd = [lax.rsqrt(means[B + b : B + b + 1] - mean[b] * mean[b] + EPS) for b in range(B)]
     line = lax.broadcasted_iota(jnp.int32, (PADROWS, CP), 0)
     rows_kept = jnp.where(line < OWN, keep[0], jnp.where(line < OWN + H, 1.0, keep[1]))
 
-    def activate(b, wq, side_kept):
+    def activate(b, wq, side_kept, n):
         mul = rstd[b] * gain
         normed = lt[0, b, wq] * mul + (bias - mean[b] * mul)
         sig = jax.nn.sigmoid(normed)
-        t80[...] = normed * sig * (rows_kept * side_kept)
+        t80[n] = normed * sig * (rows_kept * side_kept)
 
         def put(at, wide, value):
             xx[b, wq, :, at : at + wide] = value.astype(bf16)
 
-        pack_taps(put, *(t80[TOP + k : TOP + k + H, :] for k in range(3)))
+        pack_taps(put, *(t80[n, TOP + k : TOP + k + H, :] for k in range(3)))
         return normed, sig
 
-    halves = []
+    def own_columns(i, _):
+        for b in range(B):
+            for n in range(2):
+                w = i * 2 + n
+                normed, sig = activate(b, w + 1, 1.0, b * 2 + n)
+                normed, sig = normed[OWN : OWN + H], sig[OWN : OWN + H]
+                slope[b, w] = sig * (1.0 + normed * (1.0 - sig))
+        return 0
+
+    lax.fori_loop(0, W // 2, own_columns, 0)
     for b in range(B):
-
-        def own_column(w, carry):
-            normed, sig = activate(b, w + 1, 1.0)
-            normed, sig = normed[OWN : OWN + H], sig[OWN : OWN + H]
-            dn = da[b, w] * sig * (1.0 + normed * (1.0 - sig))
-            da[b, w] = dn
-            xhat = (lt[0, b, w + 1, OWN : OWN + H, :] - mean[b]) * rstd[b]
-            return (
-                carry[0] + jnp.sum(dn.reshape(H // 8, 8, CP), axis=0),
-                carry[1] + jnp.sum((dn * xhat).reshape(H // 8, 8, CP), axis=0),
-            )
-
-        z = jnp.zeros((8, CP), f32)
-        halves.append([jnp.sum(o, axis=0, keepdims=True) for o in lax.fori_loop(0, W, own_column, (z, z))])
-    a2[ia] = jnp.concatenate(
-        [halves[0][0], halves[1][0], halves[0][1], halves[1][1], gsum[0], gsum[1], jnp.zeros((2, CP), f32)], axis=0
-    )
-    exchange(a2, ia, 2, peer_a, NA)
-    for b in range(B):
-        activate(b, 0, keep[2])
-        activate(b, 9, keep[3])
+        activate(b, 0, keep[2], b * 2)
+        activate(b, 9, keep[3], b * 2 + 1)
 
     per = PL // 128
     for kw in range(3):
@@ -347,6 +349,14 @@
     lax.fori_loop(0, X, to_partner, 0)
     first = send(sb1, r1, s1_s.at[0], s1_r.at[0], dev(co_=1 - co))
 
+    def dacts(i, _):
+        b, w = i // 2, lax.rem(i, 2) * 4
+        acc = dot_nt(gx[b, pl.ds(w, 4)].reshape(4 * H, KP), wt[0])
+        for kw in range(1, 3):
+            acc = acc + dot_nt(gx[b, pl.ds(w + kw, 4)].reshape(4 * H, KP), wt[kw])
+        da[b, pl.ds(w, 4)] = widen(acc).reshape(4, H, CP)
+        return 0
+
     def conv(b):
         def body(i, _):
             w = i * 4
@@ -369,7 +379,7 @@
         out.start()
         return out
 
-    stores = [conv(0)]
+    lax.fori_loop(0, B, dacts, 0)
     first.wait_recv()
 
     def halve(i, _):
@@ -379,20 +389,89 @@
         return 0
 
     lax.fori_loop(0, X, halve, 0)
-    second = []
-    for dx in range(X):
-        for dy in range(Y):
-            if dx or dy:
-                px, py = lax.rem(x + dx, X), lax.rem(y + dy, Y)
-                k = dx * Y + dy
-                second.append(send(sb2.at[px, pl.ds(py * RBZ, RBZ)], r2.at[k], s2_s.at[k], s2_r.at[k], dev(x_=px, y_=py)))
+    T = 3
+    CH = PL // T
+    second = [[] for _ in range(T)]
+    for t in range(T):
+        lanes = pl.ds(t * CH, CH)
+        for dx in range(X):
+            for dy in range(Y):
+                if dx or dy:
+                    px, py = lax.rem(x + dx, X), lax.rem(y + dy, Y)
+                    k = dx * Y + dy
+                    second[t].append(
+                        send(
+                            sb2.at[px, pl.ds(py * RBZ, RBZ), :, lanes], r2.at[k, :, :, lanes],
+                            s2_s.at[t, k], s2_r.at[t, k], dev(x_=px, y_=py),
+                        )
+                    )
+    lax.fori_loop(B, 2 * B, dacts, 0)
+    halves = []
+    for b in range(B):
+
+        def own_column(i, carry):
+            s1, s2 = carry
+            for n in range(2):
+                w = i * 2 + n
+                dn = da[b, w] * slope[b, w]
+                da[b, w] = dn
+                xhat = (lt[0, b, w + 1, OWN : OWN + H, :] - mean[b]) * rstd[b]
+                s1 = s1 + jnp.sum(dn.reshape(H // 8, 8, CP), axis=0)
+                s2 = s2 + jnp.sum((dn * xhat).reshape(H // 8, 8, CP), axis=0)
+            return s1, s2
+
+        z = jnp.zeros((8, CP), f32)
+        halves.append([jnp.sum(o, axis=0, keepdims=True) for o in lax.fori_loop(0, W // 2, own_column, (z, z))])
+    a2[ia] = pack_groups(stacked([halves[0][0] * gain, halves[1][0] * gain, halves[0][1] * gain, halves[1][1] * gain], 8))
+    exchange(a2, ia, 2, peer_a, NA)
+    a3[ia] = stacked([halves[0][0] + halves[1][0], halves[0][1] + halves[1][1], gsum[0], gsum[1]], 4)
+    exchange(a3, ia, 4, peer_a, NA)
+    stores = [conv(0)]
     b2[ib] = gather_sum(a2, ia, 2, peer_a, NA)
     exchange(b2, ib, 3, peer_b, NB)
+    b3[ib] = gather_sum(a3, ia, 4, peer_a, NA)
+    exchange(b3, ib, 5, peer_b, NB)
+
+    def over_z(t):
+        lanes = slice(t * CH, (t + 1) * CH)
+        for cp in second[t]:
+            cp.wait_recv()
+        mine = wg[co * X + x, pl.ds(pl.multiple_of(y * (RBZ * 8), 8), RBZ * 8), lanes].reshape(RBZ, 8, CH)
+        for k in range(1, NB):
+            mine = mine + r2[k, :, :, lanes].astype(f32)
+        sb3[:, :, lanes] = mine.astype(bf16)
+        for k in range(1, NZ):
+            j, d = peer_z(k)
+            send(
+                sb3.at[pl.ds(lax.rem(j, ZL) * RB, RB), :, lanes], r3.at[iz, :, :, lanes], s3_s.at[t, k], s3_r.at[t, iz], d
+            )
+        r3[iz, :, :, lanes] = sb3[pl.ds(zl * RB, RB), :, lanes]
+
+    def to_holders(t):
+        lanes = slice(t * CH, (t + 1) * CH)
+        for k in range(1, NZ):
+            j, d = peer_z(k)
+            part = r3.at[j, :, :, lanes]
+            pltpu.make_async_remote_copy(
+                src_ref=part, dst_ref=part, send_sem=s3_s.at[t, k], recv_sem=s3_r.at[t, j], device_id=d, device_id_type=MESH
+            ).wait_recv()
+        total = r3[0, :, :, lanes].astype(f32)
+        for j in range(1, NZ):
+            total = total + r3[j, :, :, lanes].astype(f32)
+        agb[ip, :, :, lanes] = total.astype(bf16)
+        for k in range(1, NP):
+            part = agb.at[ip, :, :, lanes]
+            send(part, part, ag_s.at[t, k], ag_r.at[t, ip], peer_p(k)[1])
+
+    over_z(0)
     stores.append(conv(1))
-
-    totals = gather_sum(b2, ib, 3, peer_b, NB)
-    weights = jnp.concatenate([totals[0:4] * gain, jnp.zeros((4, CP), f32)], axis=0)
-    groups = group_sums(weights) / count
+    over_z(1)
+    over_z(2)
+    to_holders(0)
+    to_holders(1)
+
+    groups = spread_groups(gather_sum(b2, ib, 3, peer_b, NB)) / count
+    totals = gather_sum(b3, ib, 5, peer_b, NB)
     for b in range(B):
         m1, m2 = groups[b : b + 1, 0:C], groups[B + b : B + b + 1, 0:C]
         mb, rb = mean[b][:, 0:C], rstd[b][:, 0:C]
@@ -410,39 +489,25 @@
         out = pltpu.make_async_copy(og.at[b], ig_hbm.at[b], st_sem.at[B + b])
         out.start()
         stores.append(out)
-    st_ref[...] = jnp.concatenate(
-        [totals[2:3] + totals[3:4], totals[0:1] + totals[1:2], totals[4:5] + totals[5:6], jnp.zeros((5, CP), f32)], axis=0
-    )[:, 0:C] * scale
-    gs_ref[...] = jnp.concatenate([totals[4:6], jnp.zeros((6, CP), f32)], axis=0)[:, 0:C]
-
-    for cp in second:
-        cp.wait_recv()
-    mine = wg[co * X + x, pl.ds(pl.multiple_of(y * (RBZ * 8), 8), RBZ * 8), :].reshape(RBZ, 8, PL)
-    for k in range(1, NB):
-        mine = mine + r2[k].astype(f32)
-    sb3[...] = mine.astype(bf16)
-    for k in range(1, NZ):
-        j, d = peer_z(k)
-        send(sb3.at[pl.ds(lax.rem(j, ZL) * RB, RB)], r3.at[iz], s3_s.at[k], s3_r.at[iz], d)
-    r3[iz] = sb3[pl.ds(zl * RB, RB)]
-    for k in range(1, NZ):
-        j, d = peer_z(k)
-        pltpu.make_async_remote_copy(
-            src_ref=r3.at[j], dst_ref=r3.at[j], send_sem=s3_s.at[k], recv_sem=s3_r.at[j], device_id=d, device_id_type=MESH
-        ).wait_recv()
-    total = r3[0].astype(f32)
-    for j in range(1, NZ):
-        total = total + r3[j].astype(f32)
-    agb[ip] = total.astype(bf16)
-    for k in range(1, NP):
-        send(agb.at[ip], agb.at[ip], ag_s.at[k], ag_r.at[ip], peer_p(k)[1])
-    for k in range(1, NP):
-        j, d = peer_p(k)
-        pltpu.make_async_remote_copy(
-            src_ref=agb.at[j], dst_ref=agb.at[j], send_sem=ag_s.at[k], recv_sem=ag_r.at[j], device_id=d, device_id_type=MESH
-        ).wait_recv()
+    st_ref[...] = (stacked([totals[1:2], totals[0:1], totals[2:3] + totals[3:4]], 8) * scale)[:, 0:C]
+    gs_ref[...] = stacked([totals[2:3], totals[3:4]], 8)[:, 0:C]
+
+    to_holders(2)
+    for t in range(T):
+        lanes = slice(t * CH, (t + 1) * CH)
+        for k in range(1, NP):
+            j, d = peer_p(k)
+            part = agb.at[j, :, :, lanes]
+            pltpu.make_async_remote_copy(
+                src_ref=part, dst_ref=part, send_sem=ag_s.at[t, k], recv_sem=ag_r.at[t, j], device_id=d, device_id_type=MESH
+            ).wait_recv()
     for p in range(NP):
-        cwg_ref[:, p * PL : (p + 1) * PL] = agb[p].astype(f32).reshape(RB * 8, PL) * scale
+        wide[:, p * PL : (p + 1) * PL] = agb[p].astype(f32).reshape(RB * 8, PL) * scale
+    for kw in range(3):
+        at = kw * KP
+        cwg_ref[0, kw] = wide[:, at : at + C]
+        cwg_ref[1, kw] = pltpu.roll(wide[:, at + 256 : at + 640], CP - 64, 1)[:, 0:C]
+        cwg_ref[2, kw] = wide[:, at + 2 * C : at + 3 * C]
     for cp in sends:
         cp.wait_send()
     for cp in stores:
@@ -464,7 +529,7 @@
         out_shape=(
             jax.ShapeDtypeStruct((B, H, W, C), bf16),
             jax.ShapeDtypeStruct((B, H, W, C), f32),
-            jax.ShapeDtypeStruct((RB * 8, 3 * KP), f32),
+            jax.ShapeDtypeStruct((3, 3, RB * 8, C), f32),
             jax.ShapeDtypeStruct((8, C), f32),
             jax.ShapeDtypeStruct((8, C), f32),
             jax.ShapeDtypeStruct((8, TE), f32),
@@ -476,14 +541,14 @@
             V((3, 3, C, C), bf16),
             V((C, TE), bf16),
             V((TE, TE), bf16),
-            V((TE, C), bf16),
+            V((C, TE), bf16),
             V((2, 2, B, W, C), bf16),
             V((2, 2, B, H, C), bf16),
             V((2, 2, B, H, C), bf16),
             V((4, 8, CP), f32),
             V((4, 8, CP), f32),
             V((2, B, 10, PADROWS, CP), f32),
-            V((PADROWS, CP), f32),
+            V((4, PADROWS, CP), f32),
             V((B, 10, H, KP), bf16),
             V((B, 10, H, KP), bf16),
             V((3, KP, C), bf16),
@@ -499,32 +564,36 @@
             V((ZL * RB, 8, PL), bf16),
             V((NZ, RB, 8, PL), bf16),
             V((NP, RB, 8, PL), bf16),
-            V((NA, 8, CP), f32),
-            V((NB, 8, CP), f32),
-            V((NA, 8, CP), f32),
-            V((NB, 8, CP), f32),
+            V((RB * 8, 3 * KP), f32),
+            V((B, W, H, CP), f32),
+            V((NA, 1, 128), f32),
+            V((NB, 1, 128), f32),
+            V((NA, 1, 128), f32),
+            V((NB, 1, 128), f32),
+            V((NA, 4, CP), f32),
+            V((NB, 4, CP), f32),
             V((B, H, W, C), bf16),
             V((B, H, W, C), f32),
             D((6,)),
             D((2 * B,)),
             D((12,)),
             D((12,)),
-            D((4, NG)),
-            D((4, NG)),
+            D((6, NG)),
+            D((6, NG)),
             D((1,)),
             D((1,)),
-            D((NB,)),
-            D((NB,)),
-            D((NZ,)),
-            D((NZ,)),
-            D((NP,)),
-            D((NP,)),
+            D((3, NB)),
+            D((3, NB)),
+            D((3, NZ)),
+            D((3, NZ)),
+            D((3, NP)),
+            D((3, NP)),
         ],
         compiler_params=pltpu.CompilerParams(collective_id=0, has_side_effects=True, vmem_limit_bytes=62 * 1024 * 1024),
         name="block",
-    )(timestep, gain, bias, conv_b, latent, cotangent, conv_w, embed_in, embed_out, time_w)
+    )(timestep, gain, bias, conv_b, latent, cotangent, conv_w, embed_in, embed_out, time_w.T)
     scale = 1.0 / math.sqrt(B * H * Y * ZL * W * X * ZH * CO)
-    conv_w_grad = cwg.reshape(RB * 8, 3, KP)[:, :, : 3 * C].reshape(RB * 8, 3, 3, C).transpose(0, 2, 1, 3)
+    conv_w_grad = cwg.transpose(2, 0, 1, 3)
     time_w_grad = lax.dot_general(emb[0:B], gs[0:B], (((0,), (0,)), ((), ()))) * scale
     return bo, ig, conv_w_grad, st[0], st[1], st[2], time_w_grad
 

time: 85.4 us -> 65.6 us (0.77)
  Pallas kernels: 74.4 us -> 57.7 us
  local copies, waits for them, and re-layouts: 8.47 us -> 4.59 us
    pallas_call x1, Pallas kernels: 74.4 us -> 57.7 us  [step(): pl.pallas_call(functools.partial(kernel, sizes, H), out_shape=(jax.ShapeD...]
    unnamed x12 -> x9, local copies, waits for them, and re-layouts: 5.09 us -> 3.1 us
    reshape x2 -> x0, local copies, waits for them, and re-layouts: 1.67 us -> none  [step(): cwg.reshape(RB * 8, 3, KP)[:, :, :3 * C].reshape(RB * 8, 3, 3, C)]
where the time goes in v2:
time: 65.6 us; the launch traced here: 65.3 us
  Pallas kernels  57.7 us (88%)
  local copies, waits for them, and re-layouts  4.59 us (7%)
  matrix products  2.37 us (4%)
  between operations  0.66 us (1%)
    pallas_call x1, Pallas kernels, step(): pl.pallas_call(functools.partial(kernel, sizes, H), out_shape=(jax.ShapeD...  57.7 us
    unnamed x9, local copies, waits for them, and re-layouts  3.1 us
    dot_general x1, matrix products, step(): lax.dot_general(emb[0:B], gs[0:B], (((0,), (0,)), ((), ()))) * scale  2.37 us
    slice x1, local copies, waits for them, and re-layouts, step(): return (bo, ig, conv_w_grad, st[0], st[1], st[2], time_w_grad)  1.5 us

profile of v2, /device:TPU:1, one launch (start us, length us, event | category | flops | bytes accessed | tf_op | source)
XLA Modules:
  0.0 65.3 jit_solution(17382475594462147522)
XLA Ops:
  0.6 57.7 %block.1 = (bf16[2,64,8,320]{3,2,1,0:T(8,128)(2,1)}, f32[2,64,8,320]{3,2,1,0:T(8,128)}, f32[3,3,40,320]{3,2,1,0:T(8,128)}, f32[8,320]{1,0:T(8,128)}, f32[8,320]{1,0:T(8,128)}, /*index=5*/f32[8,1280]{1,0:T(8,128)}) custom-call(s32[2]{0:T(128)} %ts_ref.1, f32[320]{0:T(512)} %gain_ref.1, f32[320]{0:T(512)} %bias_ref.1, f32[320]{0:T(512)} %cb_ref.1, ...), custom_call_target="tpu_custom_call" | custom-call | tf_op jit(solution)/shard_map/block/pallas_call | solution.py:527
  58.4 0.0 copy-start.1
  58.4 0.0 copy-start
  58.4 1.5 %slice_reduce_fusion = (f32[320]{0:T(512)}, f32[320]{0:T(512)}, f32[320]{0:T(512)}) fusion(f32[8,320]{1,0:T(8,128)} %get-tuple-element.16), kind=kLoop, calls=%fused_computation.3 | loop fusion | bytes 7680 | tf_op jit(solution)/shard_map/slice | solution.py:598
  59.9 2.4 %convolution_multiply_fusion = f32[1280,320]{0,1:T(8,128)} fusion(f32[8,1280]{1,0:T(8,128)} %get-tuple-element.17, f32[8,320]{1,0:T(8,128)} %get-tuple-element.18), kind=kOutput, calls=%fused_computation | convolution fusion | flops 2048000 | bytes 1645056 | tf_op jit(solution)/shard_map/dot_general | solution.py:597
  62.2 0.0 copy-done.1
  62.2 0.9 %copy.20 = bf16[2,64,8,320]{3,2,1,0:T(8,128)(2,1)} copy(bf16[2,64,8,320]{3,2,1,0:T(8,128)(2,1)S(1)} %copy-done.1) | data formatting | bytes 1310720
  63.1 0.0 copy-done
  63.1 0.0 copy-start.2
  63.1 1.1 %copy.21 = f32[2,64,8,320]{3,2,1,0:T(8,128)} copy(f32[2,64,8,320]{3,2,1,0:T(8,128)S(1)} %copy-done) | data formatting | bytes 2621440
  64.3 0.3 copy-done.2
  64.5 0.8 %copy.22 = f32[40,3,3,320]{3,0,2,1:T(8,128)} copy(f32[40,3,3,320]{3,0,2,1:T(8,128)S(1)} %bitcast.3) | data formatting | bytes 921600
Async XLA Ops:
  58.4 3.9 %copy-start.1 = (bf16[2,64,8,320]{3,2,1,0:T(8,128)(2,1)S(1)}, bf16[2,64,8,320]{3,2,1,0:T(8,128)(2,1)}, u32[]{:S(2)}) copy-start(bf16[2,64,8,320]{3,2,1,0:T(8,128)(2,1)} %get-tuple-element.29) | copy-start | bytes 1966084
  58.4 4.8 %copy-start = (f32[2,64,8,320]{3,2,1,0:T(8,128)S(1)}, f32[2,64,8,320]{3,2,1,0:T(8,128)}, u32[]{:S(2)}) copy-start(f32[2,64,8,320]{3,2,1,0:T(8,128)} %get-tuple-element.30) | copy-start | bytes 3932164
  63.1 1.4 %copy-start.2 = (f32[3,3,40,320]{3,2,1,0:T(8,128)S(1)}, f32[3,3,40,320]{3,2,1,0:T(8,128)}, u32[]{:S(2)}) copy-start(f32[3,3,40,320]{3,2,1,0:T(8,128)} %get-tuple-element.15) | copy-start | bytes 1382404

commit v3 on v2

--- a/solution.py
+++ b/solution.py
@@ -22,6 +22,8 @@
 KP = 1024
 f32, bf16 = jnp.float32, jnp.bfloat16
 MESH = pl.DeviceIdType.MESH
+HELD = pltpu.VMEM
+LIMIT = 50 * 1024 * 1024
 
 
 def widen(v):
@@ -79,23 +81,24 @@
 def kernel(
     sizes,
     H,
-    ts_ref, gain_ref, bias_ref, cb_ref, lat_hbm, cot_hbm, cw_hbm, ein_hbm, eout_hbm, tw_hbm,
-    bo_hbm, ig_hbm, cwg_ref, st_ref, gs_ref, emb_ref,
+    ts_hbm, gain_hbm, bias_hbm, cb_hbm, lat_hbm, cot_hbm, cw_hbm, ein_hbm, eout_hbm, tw_hbm,
+    ob, og, cwg_ref, st_ref, twg_ref,
+    ts_ref, gain_ref, bias_ref, cb_ref,
     in_v, cw_v, ein_v, eout_v, tw_v,
     row_in, col_out, col_in, cor_out, cor_in,
-    lt, t80, gx, xx, wf, wt, da, co_v, gt, wg,
-    sb1, r1, sb2, r2, sb3, r3, agb, wide, slope,
-    a1, b1, a2, b2, a3, b3, ob, og,
-    ld_sem, st_sem, halo_s, halo_r, ar_s, ar_r, s1_s, s1_r, s2_s, s2_r, s3_s, s3_r, ag_s, ag_r,
+    lt, t80, gx, xx, wf, wt, da, co_v, gt, wg, wg2, wg3, wg4,
+    sb1, r1, sb2, rx, ry, ux, uy, vx, vy, sb3, r3, agb, slope,
+    a1, b1, a2, b2, a3, b3,
+    ld_sem, halo_s, halo_r, ar_s, ar_r, s1_s, s1_r, x_s, x_r, y_s, y_r, x2_s, x2_r, y2_s, y2_r, s3_s, s3_r, ag_s, ag_r,
 ):
     Y, ZL, X, ZH, CO = sizes
     y, zl, x, zh, co = (lax.axis_index(a) for a in AXES)
     row, col = y * ZL + zl, (x * ZH + zh) * CO + co
     NR, NC = Y * ZL, X * ZH * CO
     NA, NB, NP, NZ = ZH * ZL * CO, X * Y, CO * X, ZH * ZL
-    PL = 3 * KP // NP
+    HALF = KP // CO
+    CH = HALF // X
     RB = 40 // NR
-    RBZ = ZL * RB
     count = float(GROUP * H * NR * W * NC)
     scale = 1.0 / math.sqrt(B * H * NR * W * NC)
 
@@ -133,14 +136,12 @@
     left, right = lax.rem(col + NC - 1, NC), lax.rem(col + 1, NC)
     near = [dev_at(r, c) for r in (up, row, down) for c in (left, col, right) if not (r is row and c is col)]
 
-    loads = [
-        pltpu.make_async_copy(s, d, ld_sem.at[i])
-        for i, (s, d) in enumerate(
-            ((lat_hbm, in_v.at[0]), (cot_hbm, in_v.at[1]), (cw_hbm, cw_v), (ein_hbm, ein_v), (eout_hbm, eout_v), (tw_hbm, tw_v))
-        )
-    ]
-    for cp in loads:
-        cp.start()
+    pairs = (
+        (lat_hbm, in_v.at[0]), (ts_hbm, ts_ref), (gain_hbm, gain_ref), (bias_hbm, bias_ref), (cb_hbm, cb_ref),
+        (cot_hbm, in_v.at[1]), (cw_hbm, cw_v), (ein_hbm, ein_v), (eout_hbm, eout_v), (tw_hbm, tw_v),
+    )
+    loads = [pltpu.make_async_copy(s, d, ld_sem.at[i]) for i, (s, d) in enumerate(pairs)]
+    loads[0].start()
     barrier = pltpu.get_barrier_semaphore()
     greeted = (
         [peer_a(k)[1] for k in range(1, NA)]
@@ -159,27 +160,33 @@
         sends.append(cp)
         return cp
 
-    def zero(i, _):
-        lt[i // (B * 10), lax.rem(i // 10, B), lax.rem(i, 10)] = jnp.zeros((PADROWS, CP), f32)
-        return 0
-
-    lax.fori_loop(0, 2 * B * 10, zero, 0)
-    t80[...] = jnp.zeros_like(t80)
-
-    def turn(arr, b, squares):
+    for cp in loads[1:5]:
+        cp.start()
+
+    def add_up(arr, b, squares):
         def body(i, carry):
-            h = pl.multiple_of(i * 8, 8)
-            v = in_v[arr, b, pl.ds(h, 8)].astype(f32)
-            lt[arr, b, 1:9, pl.ds(h + OWN, 8), 0:C] = jnp.transpose(v, (1, 0, 2))
+            h = pl.multiple_of(i * 16, 16)
+            v = in_v[arr, b, pl.ds(h, 16)].astype(f32)
             s = carry[0] + jnp.sum(v, axis=0)
             return (s, carry[1] + jnp.sum(v * v, axis=0)) if squares else (s,)
 
         z = jnp.zeros((W, C), f32)
-        out = lax.fori_loop(0, H // 8, body, (z, z) if squares else (z,))
+        out = lax.fori_loop(0, H // 16, body, (z, z) if squares else (z,))
         return [widen(jnp.sum(o, axis=0, keepdims=True)) for o in out]
 
+    def turn(arr):
+        def body(i, _):
+            h = pl.multiple_of(i * 8, 8)
+            for b in range(B):
+                lt[arr, b, 1:9, pl.ds(h + OWN, 8), 0:C] = jnp.transpose(in_v[arr, b, pl.ds(h, 8)].astype(f32), (1, 0, 2))
+            return 0
+
+        lax.fori_loop(0, H // 8, body, 0)
+
     loads[0].wait()
-    sums = [turn(0, b, True) for b in range(B)]
+    for cp in loads[5:]:
+        cp.start()
+    sums = [add_up(0, b, True) for b in range(B)]
     a1[ia] = pack_groups(stacked([sums[0][0], sums[1][0], sums[0][1], sums[1][1]], 8))
 
     pl.semaphore_wait(barrier, len(greeted))
@@ -201,33 +208,44 @@
 
     exchange(a1, ia, 0, peer_a, NA)
 
-    halos = []
-
-    def halo(src, dst, i, d):
-        halos.append(send(src, dst, halo_s.at[i], halo_r.at[i], d))
-
-    loads[1].wait()
-    for arr in range(2):
-        halo(in_v.at[arr, :, H - 1], row_in.at[0, arr], arr, dev_at(down, col))
-        halo(in_v.at[arr, :, 0], row_in.at[1, arr], 2 + arr, dev_at(up, col))
-    gsum = [turn(1, b, False)[0] for b in range(B)]
-    for arr in range(2):
+    def send_halos(arr):
+        halos = []
+
+        def halo(src, dst, d):
+            i = len(halos)
+            halos.append(send(src, dst, halo_s.at[arr, i], halo_r.at[arr, i], d))
+
+        halo(in_v.at[arr, :, H - 1], row_in.at[0, arr], dev_at(down, col))
+        halo(in_v.at[arr, :, 0], row_in.at[1, arr], dev_at(up, col))
+        turn(arr)
         for b in range(B):
             col_out[0, arr, b] = lt[arr, b, 1, OWN : OWN + H, 0:C].astype(bf16)
             col_out[1, arr, b] = lt[arr, b, W, OWN : OWN + H, 0:C].astype(bf16)
-            for r in range(2):
-                for c in range(2):
-                    i = OWN + (H - 1) * r
-                    k = arr * B + b
-                    cor_out[2 * r + c, k : k + 1, :] = lt[arr, b, 1 + (W - 1) * c, i : i + 1, :]
-    for arr in range(2):
-        halo(col_out.at[1, arr], col_in.at[0, arr], 4 + arr, dev_at(row, right))
-        halo(col_out.at[0, arr], col_in.at[1, arr], 6 + arr, dev_at(row, left))
-    for r in range(2):
-        for c in range(2):
-            halo(cor_out.at[2 * r + c], cor_in.at[2 * (1 - r) + 1 - c], 8 + 2 * r + c, dev_at((up, down)[r], (left, right)[c]))
-
-    loads[2].wait()
+        halo(col_out.at[1, arr], col_in.at[0, arr], dev_at(row, right))
+        halo(col_out.at[0, arr], col_in.at[1, arr], dev_at(row, left))
+        for r in range(2):
+            for c in range(2):
+                i = OWN + (H - 1) * r
+                for b in range(B):
+                    cor_out[arr, 2 * r + c, b : b + 1, :] = lt[arr, b, 1 + (W - 1) * c, i : i + 1, :]
+                halo(cor_out.at[arr, 2 * r + c], cor_in.at[arr, 2 * (1 - r) + 1 - c], dev_at((up, down)[r], (left, right)[c]))
+        return halos
+
+    def zero(i, _):
+        for arr in range(2):
+            for b in range(B):
+                lt[arr, b, i, 0:OWN, :] = jnp.zeros((OWN, CP), f32)
+                lt[arr, b, i, OWN + H :, :] = jnp.zeros((PADROWS - OWN - H, CP), f32)
+                lt[arr, b, i, OWN : OWN + H, C:CP] = jnp.zeros((H, CP - C), f32)
+        return 0
+
+    lax.fori_loop(0, 10, zero, 0)
+    halos_x = send_halos(0)
+    loads[5].wait()
+    halos_g = send_halos(1)
+    gsum = [add_up(1, b, False)[0] for b in range(B)]
+
+    loads[6].wait()
     for kw in range(3):
         for kh in range(3):
             wf[kw, kh * C : (kh + 1) * C, :] = cw_v[kh, kw]
@@ -253,7 +271,7 @@
     b1[ib] = gather_sum(a1, ia, 0, peer_a, NA)
     exchange(b1, ib, 1, peer_b, NB)
 
-    for cp in loads[3:]:
+    for cp in loads[1:5] + loads[7:]:
         cp.wait()
     lane = lax.broadcasted_iota(jnp.int32, (8, C), 1)
     step = jnp.where(lane < C // 2, lane, lane - C // 2).astype(f32)
@@ -263,18 +281,18 @@
     sinus = jnp.where(lane < C // 2, jnp.cos(angle), jnp.sin(angle)).astype(bf16)
     hidden = jax.nn.silu(dot(sinus, ein_v[...])).astype(bf16)
     emb = jax.nn.silu(dot(hidden, eout_v[...])).astype(bf16)
-    emb_ref[...] = emb.astype(f32)
     temb = dot_nt(emb, tw_v[...]) + cb_ref[...].reshape(1, C)
 
-    for cp in halos:
-        cp.wait_recv()
     keep = [
         jnp.where(row > 0, 1.0, 0.0),
         jnp.where(row < NR - 1, 1.0, 0.0),
         jnp.where(col > 0, 1.0, 0.0),
         jnp.where(col < NC - 1, 1.0, 0.0),
     ]
-    for arr in range(2):
+
+    def land(arr, halos):
+        for cp in halos:
+            cp.wait_recv()
         for b in range(B):
             for side in range(2):
                 at = OWN + H if side else TOP
@@ -283,8 +301,9 @@
                     lt[arr, b, w + 1, at : at + 1, 0:C] = v[w : w + 1]
                 lt[arr, b, 9 * side, OWN : OWN + H, 0:C] = col_in[side, arr, b].astype(f32) * keep[2 + side]
                 for c in range(2):
-                    k = arr * B + b
-                    lt[arr, b, 9 * c, at : at + 1, :] = cor_in[2 * side + c, k : k + 1, :] * keep[side] * keep[2 + c]
+                    lt[arr, b, 9 * c, at : at + 1, :] = cor_in[arr, 2 * side + c, b : b + 1, :] * keep[side] * keep[2 + c]
+
+    land(0, halos_x)
 
     def build_g(i, _):
         for b in range(B):
@@ -296,8 +315,6 @@
 
                 pack_taps(put, *(lt[1, b, wq, TOP + k : TOP + k + H, :] for k in range(3)))
         return 0
-
-    lax.fori_loop(0, 5, build_g, 0)
 
     means = spread_groups(gather_sum(b1, ib, 1, peer_b, NB)) / count
     gain, bias = widen(gain_ref[...].reshape(1, C)), widen(bias_ref[...].reshape(1, C))
@@ -332,22 +349,64 @@
         activate(b, 0, keep[2], b * 2)
         activate(b, 9, keep[3], b * 2 + 1)
 
-    per = PL // 128
-    for kw in range(3):
-        for n in range(4):
-            r = dot(gt[0, 0:C], xx[0, kw : kw + W, :, n * 256 : (n + 1) * 256].reshape(W * H, 256))
-            r = r + dot(gt[1, 0:C], xx[1, kw : kw + W, :, n * 256 : (n + 1) * 256].reshape(W * H, 256))
-            for t in range(2):
-                tile = kw * 8 + n * 2 + t
-                at = tile % per * 128
-                wg[tile // per, :, at : at + 128] = r[:, t * 128 : (t + 1) * 128]
-
-    def to_partner(i, _):
-        sb1[i] = wg[(1 - co) * X + i].reshape(40, 8, PL).astype(bf16)
-        return 0
-
-    lax.fori_loop(0, X, to_partner, 0)
-    first = send(sb1, r1, s1_s.at[0], s1_r.at[0], dev(co_=1 - co))
+    T = 3
+
+    def third(half, kw):
+        lanes = pl.ds(pl.multiple_of(half * HALF, HALF), HALF)
+        r = dot(gt[0, 0:C], xx[0, kw : kw + W, :, lanes].reshape(W * H, HALF))
+        return r + dot(gt[1, 0:C], xx[1, kw : kw + W, :, lanes].reshape(W * H, HALF))
+
+    first = []
+    for t in range(T):
+        sb1[t] = third(1 - co, t).reshape(40, 8, HALF).astype(bf16)
+        first.append(send(sb1.at[t], r1.at[t], s1_s.at[t], s1_r.at[t], dev(co_=1 - co)))
+    for t in range(T):
+        wg[t] = third(co, t)
+
+    later = {}
+
+    def to_row(t):
+        first[t].wait_recv()
+        for i in range(X):
+            lanes = slice(i * CH, (i + 1) * CH)
+            v = (wg[t, :, lanes].reshape(40, 8, CH) + r1[t, :, :, lanes].astype(f32)).reshape(Y, ZL, RB, 8, CH)
+            wg2[t, i] = v
+            sb2[t, i] = v.astype(bf16)
+        later["x", t], later["y", t] = [], []
+        for k in range(1, X):
+            j = lax.rem(x + k, X)
+            later["x", t].append(send(sb2.at[t, j, :, 0], rx.at[t, k], x_s.at[t, k], x_r.at[t, k], dev(x_=j)))
+        for k in range(1, Y) if ZL > 1 else ():
+            j = lax.rem(y + k, Y)
+            later["y", t].append(send(sb2.at[t, :, j, 1], ry.at[t, k], y_s.at[t, k], y_r.at[t, k], dev(y_=j)))
+
+    def to_other(t):
+        for cp in later["x", t] + later["y", t]:
+            cp.wait_recv()
+        v = wg2[t, x, :, 0]
+        for k in range(1, X):
+            v = v + rx[t, k].astype(f32)
+        wg3[t] = v
+        ux[t] = v.astype(bf16)
+        later["x2", t], later["y2", t] = [], []
+        for k in range(1, Y):
+            j = lax.rem(y + k, Y)
+            later["y2", t].append(send(ux.at[t, j], vx.at[t, k], y2_s.at[t, k], y2_r.at[t, k], dev(y_=j)))
+        if ZL > 1:
+            v = wg2[t, :, y, 1]
+            for k in range(1, Y):
+                v = v + ry[t, k].astype(f32)
+            wg4[t] = v
+            uy[t] = v.astype(bf16)
+            for k in range(1, X):
+                j = lax.rem(x + k, X)
+                later["x2", t].append(send(uy.at[t, j], vy.at[t, k], x2_s.at[t, k], x2_r.at[t, k], dev(x_=j)))
+
+    for t in range(T):
+        to_row(t)
+
+    land(1, halos_g)
+    lax.fori_loop(0, 5, build_g, 0)
 
     def dacts(i, _):
         b, w = i // 2, lax.rem(i, 2) * 4
@@ -375,37 +434,10 @@
             return 0
 
         lax.fori_loop(0, H // 8, emit, 0)
-        out = pltpu.make_async_copy(ob.at[b], bo_hbm.at[b], st_sem.at[b])
-        out.start()
-        return out
-
-    lax.fori_loop(0, B, dacts, 0)
-    first.wait_recv()
-
-    def halve(i, _):
-        v = wg[co * X + i] + r1[i].astype(f32).reshape(C, PL)
-        wg[co * X + i] = v
-        sb2[i] = v.reshape(40, 8, PL).astype(bf16)
-        return 0
-
-    lax.fori_loop(0, X, halve, 0)
-    T = 3
-    CH = PL // T
-    second = [[] for _ in range(T)]
-    for t in range(T):
-        lanes = pl.ds(t * CH, CH)
-        for dx in range(X):
-            for dy in range(Y):
-                if dx or dy:
-                    px, py = lax.rem(x + dx, X), lax.rem(y + dy, Y)
-                    k = dx * Y + dy
-                    second[t].append(
-                        send(
-                            sb2.at[px, pl.ds(py * RBZ, RBZ), :, lanes], r2.at[k, :, :, lanes],
-                            s2_s.at[t, k], s2_r.at[t, k], dev(x_=px, y_=py),
-                        )
-                    )
-    lax.fori_loop(B, 2 * B, dacts, 0)
+    lax.fori_loop(0, 3, dacts, 0)
+    to_other(0)
+    lax.fori_loop(3, 2 * B, dacts, 0)
+    to_other(1)
     halves = []
     for b in range(B):
 
@@ -426,49 +458,51 @@
     exchange(a2, ia, 2, peer_a, NA)
     a3[ia] = stacked([halves[0][0] + halves[1][0], halves[0][1] + halves[1][1], gsum[0], gsum[1]], 4)
     exchange(a3, ia, 4, peer_a, NA)
-    stores = [conv(0)]
+    to_other(2)
+    conv(0)
+
+    def over_z(t):
+        for cp in later["x2", t] + later["y2", t]:
+            cp.wait_recv()
+        v = wg3[t, y]
+        for k in range(1, Y):
+            v = v + vx[t, k].astype(f32)
+        sb3[t, 0] = v.astype(bf16)
+        if ZL > 1:
+            v = wg4[t, x]
+            for k in range(1, X):
+                v = v + vy[t, k].astype(f32)
+            sb3[t, 1] = v.astype(bf16)
+        for k in range(1, NZ):
+            j, d = peer_z(k)
+            send(sb3.at[t, lax.rem(j, ZL)], r3.at[t, iz], s3_s.at[t, k], s3_r.at[t, iz], d)
+        r3[t, iz] = sb3[t, zl]
+
+    def to_holders(t):
+        for k in range(1, NZ):
+            j, d = peer_z(k)
+            part = r3.at[t, j]
+            pltpu.make_async_remote_copy(
+                src_ref=part, dst_ref=part, send_sem=s3_s.at[t, k], recv_sem=s3_r.at[t, j], device_id=d, device_id_type=MESH
+            ).wait_recv()
+        total = r3[t, 0].astype(f32)
+        for j in range(1, NZ):
+            total = total + r3[t, j].astype(f32)
+        agb[t, ip] = total.astype(bf16)
+        for k in range(1, NP):
+            send(agb.at[t, ip], agb.at[t, ip], ag_s.at[t, k], ag_r.at[t, ip], peer_p(k)[1])
+
+    over_z(0)
+    over_z(1)
     b2[ib] = gather_sum(a2, ia, 2, peer_a, NA)
     exchange(b2, ib, 3, peer_b, NB)
     b3[ib] = gather_sum(a3, ia, 4, peer_a, NA)
     exchange(b3, ib, 5, peer_b, NB)
-
-    def over_z(t):
-        lanes = slice(t * CH, (t + 1) * CH)
-        for cp in second[t]:
-            cp.wait_recv()
-        mine = wg[co * X + x, pl.ds(pl.multiple_of(y * (RBZ * 8), 8), RBZ * 8), lanes].reshape(RBZ, 8, CH)
-        for k in range(1, NB):
-            mine = mine + r2[k, :, :, lanes].astype(f32)
-        sb3[:, :, lanes] = mine.astype(bf16)
-        for k in range(1, NZ):
-            j, d = peer_z(k)
-            send(
-                sb3.at[pl.ds(lax.rem(j, ZL) * RB, RB), :, lanes], r3.at[iz, :, :, lanes], s3_s.at[t, k], s3_r.at[t, iz], d
-            )
-        r3[iz, :, :, lanes] = sb3[pl.ds(zl * RB, RB), :, lanes]
-
-    def to_holders(t):
-        lanes = slice(t * CH, (t + 1) * CH)
-        for k in range(1, NZ):
-            j, d = peer_z(k)
-            part = r3.at[j, :, :, lanes]
-            pltpu.make_async_remote_copy(
-                src_ref=part, dst_ref=part, send_sem=s3_s.at[t, k], recv_sem=s3_r.at[t, j], device_id=d, device_id_type=MESH
-            ).wait_recv()
-        total = r3[0, :, :, lanes].astype(f32)
-        for j in range(1, NZ):
-            total = total + r3[j, :, :, lanes].astype(f32)
-        agb[ip, :, :, lanes] = total.astype(bf16)
-        for k in range(1, NP):
-            part = agb.at[ip, :, :, lanes]
-            send(part, part, ag_s.at[t, k], ag_r.at[t, ip], peer_p(k)[1])
-
-    over_z(0)
-    stores.append(conv(1))
-    over_z(1)
     over_z(2)
+    conv(1)
     to_holders(0)
     to_holders(1)
+    to_holders(2)
 
     groups = spread_groups(gather_sum(b2, ib, 3, peer_b, NB)) / count
     totals = gather_sum(b3, ib, 5, peer_b, NB)
@@ -486,31 +520,40 @@
             return 0
 
         lax.fori_loop(0, H // 8, emit, 0)
-        out = pltpu.make_async_copy(og.at[b], ig_hbm.at[b], st_sem.at[B + b])
-        out.start()
-        stores.append(out)
     st_ref[...] = (stacked([totals[1:2], totals[0:1], totals[2:3] + totals[3:4]], 8) * scale)[:, 0:C]
-    gs_ref[...] = stacked([totals[2:3], totals[3:4]], 8)[:, 0:C]
-
-    to_holders(2)
+    g2 = jnp.concatenate([totals[2:3], totals[3:4]], axis=0)[:, 0:C]
+    hi = g2.astype(bf16)
+    rest = g2 - hi.astype(f32)
+    mid = rest.astype(bf16)
+    low = (rest - mid.astype(f32)).astype(bf16)
+    e2 = emb[0:B].astype(f32)
+    left_rows = jnp.concatenate([hi.astype(f32), mid.astype(f32), low.astype(f32), jnp.zeros((2, C), f32)], axis=0)
+    right_rows = jnp.concatenate([e2, e2, e2, jnp.zeros((2, TE), f32)], axis=0).astype(bf16)
+    twg_ref[...] = dot(jnp.transpose(left_rows).astype(bf16), right_rows) * scale
+
     for t in range(T):
-        lanes = slice(t * CH, (t + 1) * CH)
         for k in range(1, NP):
             j, d = peer_p(k)
-            part = agb.at[j, :, :, lanes]
+            part = agb.at[t, j]
             pltpu.make_async_remote_copy(
                 src_ref=part, dst_ref=part, send_sem=ag_s.at[t, k], recv_sem=ag_r.at[t, j], device_id=d, device_id_type=MESH
             ).wait_recv()
-    for p in range(NP):
-        wide[:, p * PL : (p + 1) * PL] = agb[p].astype(f32).reshape(RB * 8, PL) * scale
-    for kw in range(3):
-        at = kw * KP
-        cwg_ref[0, kw] = wide[:, at : at + C]
-        cwg_ref[1, kw] = pltpu.roll(wide[:, at + 256 : at + 640], CP - 64, 1)[:, 0:C]
-        cwg_ref[2, kw] = wide[:, at + 2 * C : at + 3 * C]
+        full = jnp.concatenate([agb[t, p].astype(f32).reshape(RB * 8, CH) for p in range(NP)], axis=1) * scale
+        cwg_ref[0, t] = full[:, 0:C]
+        cwg_ref[1, t] = pltpu.roll(full[:, 256:640], CP - 64, 1)[:, 0:C]
+        cwg_ref[2, t] = full[:, 2 * C : 3 * C]
     for cp in sends:
         cp.wait_send()
-    for cp in stores:
+
+
+def write_out(ob, og, cwg, st, twg, bo_hbm, ig_hbm, cwg_hbm, twg_hbm, gg_ref, bg_ref, cbg_ref, sem):
+    pairs = ((twg, twg_hbm), (og, ig_hbm), (ob, bo_hbm), (cwg, cwg_hbm))
+    copies = [pltpu.make_async_copy(s, d, sem.at[i]) for i, (s, d) in enumerate(pairs)]
+    for cp in copies:
+        cp.start()
+    for i, ref in enumerate((gg_ref, bg_ref, cbg_ref)):
+        ref[...] = st[i : i + 1, :].reshape(C)
+    for cp in copies:
         cp.wait()
 
 
@@ -518,25 +561,30 @@
     Y, ZL, X, ZH, CO = sizes
     H = latent.shape[1]
     NA, NB, NP, NZ = ZH * ZL * CO, X * Y, CO * X, ZH * ZL
-    PL = 3 * KP // NP
+    HALF = KP // CO
+    CH = HALF // X
     RB = 40 // (Y * ZL)
+    T = 3
     anyspace = pl.BlockSpec(memory_space=pl.ANY)
     vmem = pl.BlockSpec(memory_space=pltpu.VMEM)
     V, D = pltpu.VMEM, pltpu.SemaphoreType.DMA
     NG = max(NA, NB)
-    bo, ig, cwg, st, gs, emb = pl.pallas_call(
+    held = pl.pallas_call(
         functools.partial(kernel, sizes, H),
         out_shape=(
-            jax.ShapeDtypeStruct((B, H, W, C), bf16),
-            jax.ShapeDtypeStruct((B, H, W, C), f32),
-            jax.ShapeDtypeStruct((3, 3, RB * 8, C), f32),
-            jax.ShapeDtypeStruct((8, C), f32),
-            jax.ShapeDtypeStruct((8, C), f32),
-            jax.ShapeDtypeStruct((8, TE), f32),
+            HELD((B, H, W, C), bf16),
+            HELD((B, H, W, C), f32),
+            HELD((3, 3, RB * 8, C), f32),
+            HELD((8, C), f32),
+            HELD((C, TE), f32),
         ),
-        in_specs=[pl.BlockSpec(memory_space=pltpu.SMEM)] + [vmem] * 3 + [anyspace] * 6,
-        out_specs=(anyspace, anyspace, vmem, vmem, vmem, vmem),
+        in_specs=[anyspace] * 10,
+        out_specs=(vmem,) * 5,
         scratch_shapes=[
+            pltpu.SMEM((B,), jnp.int32),
+            V((C,), f32),
+            V((C,), f32),
+            V((C,), f32),
             V((2, B, H, W, C), bf16),
             V((3, 3, C, C), bf16),
             V((C, TE), bf16),
@@ -545,8 +593,8 @@
             V((2, 2, B, W, C), bf16),
             V((2, 2, B, H, C), bf16),
             V((2, 2, B, H, C), bf16),
-            V((4, 8, CP), f32),
-            V((4, 8, CP), f32),
+            V((2, 4, 8, CP), f32),
+            V((2, 4, 8, CP), f32),
             V((2, B, 10, PADROWS, CP), f32),
             V((4, PADROWS, CP), f32),
             V((B, 10, H, KP), bf16),
@@ -556,15 +604,22 @@
             V((B, W, H, CP), f32),
             V((B, W, H, CP), f32),
             V((B, CP, W * H), bf16),
-            V((NP, C, PL), f32),
-            V((X, 40, 8, PL), bf16),
-            V((X, 40, 8, PL), bf16),
-            V((X, 40, 8, PL), bf16),
-            V((NB, ZL * RB, 8, PL), bf16),
-            V((ZL * RB, 8, PL), bf16),
-            V((NZ, RB, 8, PL), bf16),
-            V((NP, RB, 8, PL), bf16),
-            V((RB * 8, 3 * KP), f32),
+            V((T, C, HALF), f32),
+            V((T, X, Y, ZL, RB, 8, CH), f32),
+            V((T, Y, RB, 8, CH), f32),
+            V((T, X, RB, 8, CH), f32),
+            V((T, 40, 8, HALF), bf16),
+            V((T, 40, 8, HALF), bf16),
+            V((T, X, Y, ZL, RB, 8, CH), bf16),
+            V((T, X, Y, RB, 8, CH), bf16),
+            V((T, Y, X, RB, 8, CH), bf16),
+            V((T, Y, RB, 8, CH), bf16),
+            V((T, X, RB, 8, CH), bf16),
+            V((T, Y, RB, 8, CH), bf16),
+            V((T, X, RB, 8, CH), bf16),
+            V((T, ZL, RB, 8, CH), bf16),
+            V((T, NZ, RB, 8, CH), bf16),
+            V((T, NP, RB, 8, CH), bf16),
             V((B, W, H, CP), f32),
             V((NA, 1, 128), f32),
             V((NB, 1, 128), f32),
@@ -572,30 +627,47 @@
             V((NB, 1, 128), f32),
             V((NA, 4, CP), f32),
             V((NB, 4, CP), f32),
-            V((B, H, W, C), bf16),
-            V((B, H, W, C), f32),
-            D((6,)),
-            D((2 * B,)),
-            D((12,)),
-            D((12,)),
+            D((10,)),
+            D((2, 8)),
+            D((2, 8)),
             D((6, NG)),
             D((6, NG)),
-            D((1,)),
-            D((1,)),
-            D((3, NB)),
-            D((3, NB)),
-            D((3, NZ)),
-            D((3, NZ)),
-            D((3, NP)),
-            D((3, NP)),
+            D((T,)),
+            D((T,)),
+            D((T, X)),
+            D((T, X)),
+            D((T, Y)),
+            D((T, Y)),
+            D((T, X)),
+            D((T, X)),
+            D((T, Y)),
+            D((T, Y)),
+            D((T, NZ)),
+            D((T, NZ)),
+            D((T, NP)),
+            D((T, NP)),
         ],
-        compiler_params=pltpu.CompilerParams(collective_id=0, has_side_effects=True, vmem_limit_bytes=62 * 1024 * 1024),
+        compiler_params=pltpu.CompilerParams(collective_id=0, has_side_effects=True, vmem_limit_bytes=LIMIT),
         name="block",
     )(timestep, gain, bias, conv_b, latent, cotangent, conv_w, embed_in, embed_out, time_w.T)
-    scale = 1.0 / math.sqrt(B * H * Y * ZL * W * X * ZH * CO)
-    conv_w_grad = cwg.transpose(2, 0, 1, 3)
-    time_w_grad = lax.dot_general(emb[0:B], gs[0:B], (((0,), (0,)), ((), ()))) * scale
-    return bo, ig, conv_w_grad, st[0], st[1], st[2], time_w_grad
+    bo, ig, cwg, twg, gg, bg, cbg = pl.pallas_call(
+        write_out,
+        out_shape=(
+            jax.ShapeDtypeStruct((B, H, W, C), bf16),
+            jax.ShapeDtypeStruct((B, H, W, C), f32),
+            jax.ShapeDtypeStruct((3, 3, RB * 8, C), f32),
+            jax.ShapeDtypeStruct((C, TE), f32),
+            jax.ShapeDtypeStruct((C,), f32),
+            jax.ShapeDtypeStruct((C,), f32),
+            jax.ShapeDtypeStruct((C,), f32),
+        ),
+        in_specs=[vmem] * 5,
+        out_specs=(anyspace,) * 4 + (vmem,) * 3,
+        scratch_shapes=[D((4,))],
+        compiler_params=pltpu.CompilerParams(vmem_limit_bytes=1024 * 1024),
+        name="write_out",
+    )(*held)
+    return bo, ig, cwg.transpose(2, 0, 1, 3), gg, bg, cbg, twg.T
 
 
 def build(finer):

time: 65.6 us -> 55.6 us (0.85)
  local copies, waits for them, and re-layouts: 4.59 us -> 0 us
  Pallas kernels: 57.7 us -> 54.9 us
  matrix products: 2.37 us -> 0 us
    unnamed x9 -> x0, local copies, waits for them, and re-layouts: 3.1 us -> none
    pallas_call x1 -> x2, Pallas kernels: 57.7 us -> 54.9 us  [the longest x1 52.1 us: step(): pl.pallas_call(functools.partial(kernel, sizes, H), out_shape=(HELD((B, H...]
    dot_general x1 -> x0, matrix products: 2.37 us -> none  [step(): lax.dot_general(emb[0:B], gs[0:B], (((0,), (0,)), ((), ()))) * scale]
    slice x1 -> x0, local copies, waits for them, and re-layouts: 1.5 us -> none  [step(): return (bo, ig, conv_w_grad, st[0], st[1], st[2], time_w_grad)]
where the time goes in v3:
time: 55.6 us; the launch traced here: 55.5 us
  Pallas kernels  54.9 us (99%)
  between operations  0.64 us (1%)
    pallas_call x1, Pallas kernels, step(): pl.pallas_call(functools.partial(kernel, sizes, H), out_shape=(HELD((B, H...  52.1 us
    pallas_call x1, Pallas kernels, step(): pl.pallas_call(write_out, out_shape=(jax.ShapeDtypeStruct((B, H, W, C), b...  2.73 us

profile of v3, /device:TPU:1, one launch (start us, length us, event | category | flops | bytes accessed | tf_op | source)
XLA Modules:
  0.0 55.5 jit_solution(1046948480414837319)
XLA Ops:
  0.6 52.1 %block.1 = (bf16[2,64,8,320]{3,2,1,0:T(8,128)(2,1)S(1)}, f32[2,64,8,320]{3,2,1,0:T(8,128)S(1)}, f32[3,3,40,320]{3,2,1,0:T(8,128)S(1)}, f32[8,320]{1,0:T(8,128)S(1)}, f32[320,1280]{1,0:T(8,128)S(1)}) custom-call(s32[2]{0:T(128)} %ts_hbm.1, f32[320]{0:T(512)} %gain_hbm.1, f32[320]{0:T(512)} %bias_hbm.1, f32[320]{0:T(512)} %cb_hbm.1, ...), custom_call_target="tpu_custom_call" | custom-call | tf_op jit(solution)/shard_map/block/pallas_call | solution.py:572
  52.8 2.7 %write_out.1 = (bf16[2,64,8,320]{3,2,1,0:T(8,128)(2,1)}, f32[2,64,8,320]{3,2,1,0:T(8,128)}, f32[3,3,40,320]{3,2,1,0:T(8,128)}, f32[320,1280]{1,0:T(8,128)}, f32[320]{0:T(512)}, /*index=5*/f32[320]{0:T(512)}, f32[320]{0:T(512)}) custom-call(bf16[2,64,8,320]{3,2,1,0:T(8,128)(2,1)S(1)} %get-tuple-element.19.ob, f32[2,64,8,320]{3,2,1,0:T(8,128)S(1)} %get-tuple-element.20.og, ...), custom_call_target="tpu_custom_call" | custom-call | tf_op jit(solution)/shard_map/write_out/pallas_call | solution.py:653

commit v4 on v3

--- a/solution.py
+++ b/solution.py
@@ -88,7 +88,7 @@
     row_in, col_out, col_in, cor_out, cor_in,
     lt, t80, gx, xx, wf, wt, da, co_v, gt, wg, wg2, wg3, wg4,
     sb1, r1, sb2, rx, ry, ux, uy, vx, vy, sb3, r3, agb, slope,
-    a1, b1, a2, b2, a3, b3,
+    a1, b1, a2, b2, a3, b3, a4, b4,
     ld_sem, halo_s, halo_r, ar_s, ar_r, s1_s, s1_r, x_s, x_r, y_s, y_r, x2_s, x2_r, y2_s, y2_r, s3_s, s3_r, ag_s, ag_r,
 ):
     Y, ZL, X, ZH, CO = sizes
@@ -137,16 +137,18 @@
     near = [dev_at(r, c) for r in (up, row, down) for c in (left, col, right) if not (r is row and c is col)]
 
     pairs = (
-        (lat_hbm, in_v.at[0]), (ts_hbm, ts_ref), (gain_hbm, gain_ref), (bias_hbm, bias_ref), (cb_hbm, cb_ref),
+        (lat_hbm.at[0], in_v.at[0, 0]), (ts_hbm, ts_ref), (gain_hbm, gain_ref), (bias_hbm, bias_ref), (cb_hbm, cb_ref),
         (cot_hbm, in_v.at[1]), (cw_hbm, cw_v), (ein_hbm, ein_v), (eout_hbm, eout_v), (tw_hbm, tw_v),
+        (lat_hbm.at[1], in_v.at[0, 1]),
     )
     loads = [pltpu.make_async_copy(s, d, ld_sem.at[i]) for i, (s, d) in enumerate(pairs)]
     loads[0].start()
+    loads[10].start()
     barrier = pltpu.get_barrier_semaphore()
     greeted = (
         [peer_a(k)[1] for k in range(1, NA)]
         + [peer_b(k)[1] for k in range(1, NB)]
-        + [peer_p(k)[1] for k in range(1, NP)]
+        + [dev(x_=lax.rem(x + k, X), co_=1 - co) for k in range(1, X)]
         + near
     )
     for d in greeted:
@@ -184,23 +186,34 @@
         lax.fori_loop(0, H // 8, body, 0)
 
     loads[0].wait()
-    for cp in loads[5:]:
+    sums = [add_up(0, 0, True)]
+    loads[10].wait()
+    for cp in loads[5:10]:
         cp.start()
-    sums = [add_up(0, b, True) for b in range(B)]
+    sums.append(add_up(0, 1, True))
     a1[ia] = pack_groups(stacked([sums[0][0], sums[1][0], sums[0][1], sums[1][1]], 8))
 
     pl.semaphore_wait(barrier, len(greeted))
 
+    def fan(copies, s, r, whole):
+        for src, dst, d in copies:
+            pltpu.make_async_remote_copy(src_ref=src, dst_ref=dst, send_sem=s, recv_sem=r, device_id=d, device_id_type=MESH).start()
+        every = pltpu.make_async_remote_copy(
+            src_ref=whole, dst_ref=whole, send_sem=s, recv_sem=r, device_id=copies[0][2], device_id_type=MESH
+        )
+        sends.append(every)
+        return every
+
+    arrivals = {}
+
     def exchange(buf, own, sem, peers, n):
-        for k in range(1, n):
-            send(buf.at[own], buf.at[own], ar_s.at[sem, k], ar_r.at[sem, own], peers(k)[1])
-
-    def gather_sum(buf, own, sem, peers, n):
-        for k in range(1, n):
-            j, d = peers(k)
-            pltpu.make_async_remote_copy(
-                src_ref=buf.at[j], dst_ref=buf.at[j], send_sem=ar_s.at[sem, k], recv_sem=ar_r.at[sem, j], device_id=d, device_id_type=MESH
-            ).wait_recv()
+        part = buf.at[own]
+        arrivals[sem] = fan(
+            [(part, part, peers(k)[1]) for k in range(1, n)], ar_s.at[sem], ar_r.at[sem], buf.at[pl.ds(0, n - 1)]
+        )
+
+    def gather_sum(buf, sem, n):
+        arrivals[sem].wait_recv()
         total = buf[0]
         for j in range(1, n):
             total = total + buf[j]
@@ -268,10 +281,12 @@
             v = lt[1, b, 1 + k * part : 1 + (k + 1) * part, OWN : OWN + H, :].reshape(part * H, CP)
             gt[b, :, k * part * H : (k + 1) * part * H] = jnp.transpose(v).astype(bf16)
 
-    b1[ib] = gather_sum(a1, ia, 0, peer_a, NA)
+    b1[ib] = gather_sum(a1, 0, NA)
     exchange(b1, ib, 1, peer_b, NB)
-
-    for cp in loads[1:5] + loads[7:]:
+    a4[ia] = jnp.concatenate(gsum, axis=0)
+    exchange(a4, ia, 6, peer_a, NA)
+
+    for cp in loads[1:5] + loads[7:10]:
         cp.wait()
     lane = lax.broadcasted_iota(jnp.int32, (8, C), 1)
     step = jnp.where(lane < C // 2, lane, lane - C // 2).astype(f32)
@@ -316,7 +331,7 @@
                 pack_taps(put, *(lt[1, b, wq, TOP + k : TOP + k + H, :] for k in range(3)))
         return 0
 
-    means = spread_groups(gather_sum(b1, ib, 1, peer_b, NB)) / count
+    means = spread_groups(gather_sum(b1, 1, NB)) / count
     gain, bias = widen(gain_ref[...].reshape(1, C)), widen(bias_ref[...].reshape(1, C))
     mean = [means[b : b + 1] for b in range(B)]
     rstd = [lax.rsqrt(means[B + b : B + b + 1] - mean[b] * mean[b] + EPS) for b in range(B)]
@@ -360,8 +375,6 @@
     for t in range(T):
         sb1[t] = third(1 - co, t).reshape(40, 8, HALF).astype(bf16)
         first.append(send(sb1.at[t], r1.at[t], s1_s.at[t], s1_r.at[t], dev(co_=1 - co)))
-    for t in range(T):
-        wg[t] = third(co, t)
 
     later = {}
 
@@ -372,39 +385,47 @@
             v = (wg[t, :, lanes].reshape(40, 8, CH) + r1[t, :, :, lanes].astype(f32)).reshape(Y, ZL, RB, 8, CH)
             wg2[t, i] = v
             sb2[t, i] = v.astype(bf16)
-        later["x", t], later["y", t] = [], []
-        for k in range(1, X):
-            j = lax.rem(x + k, X)
-            later["x", t].append(send(sb2.at[t, j, :, 0], rx.at[t, k], x_s.at[t, k], x_r.at[t, k], dev(x_=j)))
-        for k in range(1, Y) if ZL > 1 else ():
-            j = lax.rem(y + k, Y)
-            later["y", t].append(send(sb2.at[t, :, j, 1], ry.at[t, k], y_s.at[t, k], y_r.at[t, k], dev(y_=j)))
+        peers = [lax.rem(x + k, X) for k in range(1, X)]
+        later["x", t] = fan(
+            [(sb2.at[t, j, :, 0], rx.at[t, k], dev(x_=j)) for k, j in enumerate(peers)],
+            x_s.at[t], x_r.at[t], rx.at[t],
+        )
+        if ZL > 1:
+            peers = [lax.rem(y + k, Y) for k in range(1, Y)]
+            later["y", t] = fan(
+                [(sb2.at[t, :, j, 1], ry.at[t, k], dev(y_=j)) for k, j in enumerate(peers)],
+                y_s.at[t], y_r.at[t], ry.at[t],
+            )
 
     def to_other(t):
-        for cp in later["x", t] + later["y", t]:
-            cp.wait_recv()
+        later["x", t].wait_recv()
         v = wg2[t, x, :, 0]
-        for k in range(1, X):
+        for k in range(X - 1):
             v = v + rx[t, k].astype(f32)
         wg3[t] = v
         ux[t] = v.astype(bf16)
-        later["x2", t], later["y2", t] = [], []
-        for k in range(1, Y):
-            j = lax.rem(y + k, Y)
-            later["y2", t].append(send(ux.at[t, j], vx.at[t, k], y2_s.at[t, k], y2_r.at[t, k], dev(y_=j)))
+        peers = [lax.rem(y + k, Y) for k in range(1, Y)]
+        later["y2", t] = fan(
+            [(ux.at[t, j], vx.at[t, k], dev(y_=j)) for k, j in enumerate(peers)], y2_s.at[t], y2_r.at[t], vx.at[t]
+        )
         if ZL > 1:
+            later["y", t].wait_recv()
             v = wg2[t, :, y, 1]
-            for k in range(1, Y):
+            for k in range(Y - 1):
                 v = v + ry[t, k].astype(f32)
             wg4[t] = v
             uy[t] = v.astype(bf16)
-            for k in range(1, X):
-                j = lax.rem(x + k, X)
-                later["x2", t].append(send(uy.at[t, j], vy.at[t, k], x2_s.at[t, k], x2_r.at[t, k], dev(x_=j)))
+            peers = [lax.rem(x + k, X) for k in range(1, X)]
+            later["x2", t] = fan(
+                [(uy.at[t, j], vy.at[t, k], dev(x_=j)) for k, j in enumerate(peers)], x2_s.at[t], x2_r.at[t], vy.at[t]
+            )
 
     for t in range(T):
+        wg[t] = third(co, t)
         to_row(t)
 
+    b4[ib] = gather_sum(a4, 6, NA)
+    exchange(b4, ib, 7, peer_b, NB)
     land(1, halos_g)
     lax.fori_loop(0, 5, build_g, 0)
 
@@ -416,17 +437,14 @@
         da[b, pl.ds(w, 4)] = widen(acc).reshape(4, H, CP)
         return 0
 
-    def conv(b):
-        def body(i, _):
-            w = i * 4
-            acc = dot(xx[b, pl.ds(w, 4)].reshape(4 * H, KP), wf[0])
-            for kw in range(1, 3):
-                acc = acc + dot(xx[b, pl.ds(w + kw, 4)].reshape(4 * H, KP), wf[kw])
-            co_v[b, pl.ds(w, 4), :, 0:C] = acc.reshape(4, H, C)
-            return 0
-
-        lax.fori_loop(0, 2, body, 0)
-
+    def conv(b, half):
+        w = half * 4
+        acc = dot(xx[b, w : w + 4].reshape(4 * H, KP), wf[0])
+        for kw in range(1, 3):
+            acc = acc + dot(xx[b, w + kw : w + kw + 4].reshape(4 * H, KP), wf[kw])
+        co_v[b, w : w + 4, :, 0:C] = acc.reshape(4, H, C)
+
+    def emit_block(b):
         def emit(i, _):
             h = pl.multiple_of(i * 8, 8)
             v = co_v[b, :, pl.ds(h, 8), 0:C] + lt[0, b, 1:9, pl.ds(h + OWN, 8), 0:C] + temb[b : b + 1]
@@ -434,10 +452,12 @@
             return 0
 
         lax.fori_loop(0, H // 8, emit, 0)
-    lax.fori_loop(0, 3, dacts, 0)
+
+    lax.fori_loop(0, 2, dacts, 0)
     to_other(0)
+    lax.fori_loop(2, 3, dacts, 0)
+    to_other(1)
     lax.fori_loop(3, 2 * B, dacts, 0)
-    to_other(1)
     halves = []
     for b in range(B):
 
@@ -456,56 +476,69 @@
         halves.append([jnp.sum(o, axis=0, keepdims=True) for o in lax.fori_loop(0, W // 2, own_column, (z, z))])
     a2[ia] = pack_groups(stacked([halves[0][0] * gain, halves[1][0] * gain, halves[0][1] * gain, halves[1][1] * gain], 8))
     exchange(a2, ia, 2, peer_a, NA)
-    a3[ia] = stacked([halves[0][0] + halves[1][0], halves[0][1] + halves[1][1], gsum[0], gsum[1]], 4)
+    a3[ia] = jnp.concatenate([halves[0][0] + halves[1][0], halves[0][1] + halves[1][1]], axis=0)
     exchange(a3, ia, 4, peer_a, NA)
     to_other(2)
-    conv(0)
+    def time_grad():
+        hi = gtotal[:, 0:C].astype(bf16)
+        rest = gtotal[:, 0:C] - hi.astype(f32)
+        mid = rest.astype(bf16)
+        low = (rest - mid.astype(f32)).astype(bf16)
+        e2 = emb[0:B].astype(f32)
+        left_rows = jnp.concatenate([hi.astype(f32), mid.astype(f32), low.astype(f32), jnp.zeros((2, C), f32)], axis=0)
+        right_rows = jnp.concatenate([e2, e2, e2, jnp.zeros((2, TE), f32)], axis=0).astype(bf16)
+        return dot(jnp.transpose(left_rows).astype(bf16), right_rows) * scale
 
     def over_z(t):
-        for cp in later["x2", t] + later["y2", t]:
-            cp.wait_recv()
+        later["y2", t].wait_recv()
         v = wg3[t, y]
-        for k in range(1, Y):
+        for k in range(Y - 1):
             v = v + vx[t, k].astype(f32)
         sb3[t, 0] = v.astype(bf16)
         if ZL > 1:
+            later["x2", t].wait_recv()
             v = wg4[t, x]
-            for k in range(1, X):
+            for k in range(X - 1):
                 v = v + vy[t, k].astype(f32)
             sb3[t, 1] = v.astype(bf16)
-        for k in range(1, NZ):
-            j, d = peer_z(k)
-            send(sb3.at[t, lax.rem(j, ZL)], r3.at[t, iz], s3_s.at[t, k], s3_r.at[t, iz], d)
+        peers = [peer_z(k) for k in range(1, NZ)]
+        later["z", t] = fan(
+            [(sb3.at[t, lax.rem(j, ZL)], r3.at[t, iz], d) for j, d in peers], s3_s.at[t], s3_r.at[t], r3.at[t, pl.ds(0, NZ - 1)]
+        )
         r3[t, iz] = sb3[t, zl]
 
     def to_holders(t):
-        for k in range(1, NZ):
-            j, d = peer_z(k)
-            part = r3.at[t, j]
-            pltpu.make_async_remote_copy(
-                src_ref=part, dst_ref=part, send_sem=s3_s.at[t, k], recv_sem=s3_r.at[t, j], device_id=d, device_id_type=MESH
-            ).wait_recv()
+        later["z", t].wait_recv()
         total = r3[t, 0].astype(f32)
         for j in range(1, NZ):
             total = total + r3[t, j].astype(f32)
         agb[t, ip] = total.astype(bf16)
-        for k in range(1, NP):
-            send(agb.at[t, ip], agb.at[t, ip], ag_s.at[t, k], ag_r.at[t, ip], peer_p(k)[1])
+        part = agb.at[t, ip]
+        later["p", t] = fan(
+            [(part, part, peer_p(k)[1]) for k in range(1, NP)], ag_s.at[t], ag_r.at[t], agb.at[t, pl.ds(0, NP - 1)]
+        )
 
     over_z(0)
+    conv(0, 0)
     over_z(1)
-    b2[ib] = gather_sum(a2, ia, 2, peer_a, NA)
+    conv(0, 1)
+    emit_block(0)
+    over_z(2)
+    conv(1, 0)
+    conv(1, 1)
+    emit_block(1)
+    b2[ib] = gather_sum(a2, 2, NA)
     exchange(b2, ib, 3, peer_b, NB)
-    b3[ib] = gather_sum(a3, ia, 4, peer_a, NA)
+    b3[ib] = gather_sum(a3, 4, NA)
     exchange(b3, ib, 5, peer_b, NB)
-    over_z(2)
-    conv(1)
     to_holders(0)
+    gtotal = gather_sum(b4, 7, NB)
+    twg_ref[...] = time_grad()
     to_holders(1)
     to_holders(2)
 
-    groups = spread_groups(gather_sum(b2, ib, 3, peer_b, NB)) / count
-    totals = gather_sum(b3, ib, 5, peer_b, NB)
+    groups = spread_groups(gather_sum(b2, 3, NB)) / count
+    totals = gather_sum(b3, 5, NB)
     for b in range(B):
         m1, m2 = groups[b : b + 1, 0:C], groups[B + b : B + b + 1, 0:C]
         mb, rb = mean[b][:, 0:C], rstd[b][:, 0:C]
@@ -520,24 +553,9 @@
             return 0
 
         lax.fori_loop(0, H // 8, emit, 0)
-    st_ref[...] = (stacked([totals[1:2], totals[0:1], totals[2:3] + totals[3:4]], 8) * scale)[:, 0:C]
-    g2 = jnp.concatenate([totals[2:3], totals[3:4]], axis=0)[:, 0:C]
-    hi = g2.astype(bf16)
-    rest = g2 - hi.astype(f32)
-    mid = rest.astype(bf16)
-    low = (rest - mid.astype(f32)).astype(bf16)
-    e2 = emb[0:B].astype(f32)
-    left_rows = jnp.concatenate([hi.astype(f32), mid.astype(f32), low.astype(f32), jnp.zeros((2, C), f32)], axis=0)
-    right_rows = jnp.concatenate([e2, e2, e2, jnp.zeros((2, TE), f32)], axis=0).astype(bf16)
-    twg_ref[...] = dot(jnp.transpose(left_rows).astype(bf16), right_rows) * scale
-
+    st_ref[...] = (stacked([totals[1:2], totals[0:1], gtotal[0:1] + gtotal[1:2]], 8) * scale)[:, 0:C]
     for t in range(T):
-        for k in range(1, NP):
-            j, d = peer_p(k)
-            part = agb.at[t, j]
-            pltpu.make_async_remote_copy(
-                src_ref=part, dst_ref=part, send_sem=ag_s.at[t, k], recv_sem=ag_r.at[t, j], device_id=d, device_id_type=MESH
-            ).wait_recv()
+        later["p", t].wait_recv()
         full = jnp.concatenate([agb[t, p].astype(f32).reshape(RB * 8, CH) for p in range(NP)], axis=1) * scale
         cwg_ref[0, t] = full[:, 0:C]
         cwg_ref[1, t] = pltpu.roll(full[:, 256:640], CP - 64, 1)[:, 0:C]
@@ -568,7 +586,6 @@
     anyspace = pl.BlockSpec(memory_space=pl.ANY)
     vmem = pl.BlockSpec(memory_space=pltpu.VMEM)
     V, D = pltpu.VMEM, pltpu.SemaphoreType.DMA
-    NG = max(NA, NB)
     held = pl.pallas_call(
         functools.partial(kernel, sizes, H),
         out_shape=(
@@ -611,12 +628,12 @@
             V((T, 40, 8, HALF), bf16),
             V((T, 40, 8, HALF), bf16),
             V((T, X, Y, ZL, RB, 8, CH), bf16),
-            V((T, X, Y, RB, 8, CH), bf16),
-            V((T, Y, X, RB, 8, CH), bf16),
+            V((T, X - 1, Y, RB, 8, CH), bf16),
+            V((T, Y - 1, X, RB, 8, CH), bf16),
             V((T, Y, RB, 8, CH), bf16),
             V((T, X, RB, 8, CH), bf16),
-            V((T, Y, RB, 8, CH), bf16),
-            V((T, X, RB, 8, CH), bf16),
+            V((T, Y - 1, RB, 8, CH), bf16),
+            V((T, X - 1, RB, 8, CH), bf16),
             V((T, ZL, RB, 8, CH), bf16),
             V((T, NZ, RB, 8, CH), bf16),
             V((T, NP, RB, 8, CH), bf16),
@@ -625,27 +642,29 @@
             V((NB, 1, 128), f32),
             V((NA, 1, 128), f32),
             V((NB, 1, 128), f32),
-            V((NA, 4, CP), f32),
-            V((NB, 4, CP), f32),
-            D((10,)),
+            V((NA, B, CP), f32),
+            V((NB, B, CP), f32),
+            V((NA, B, CP), f32),
+            V((NB, B, CP), f32),
+            D((11,)),
             D((2, 8)),
             D((2, 8)),
-            D((6, NG)),
-            D((6, NG)),
-            D((T,)),
-            D((T,)),
-            D((T, X)),
-            D((T, X)),
-            D((T, Y)),
-            D((T, Y)),
-            D((T, X)),
-            D((T, X)),
-            D((T, Y)),
-            D((T, Y)),
-            D((T, NZ)),
-            D((T, NZ)),
-            D((T, NP)),
-            D((T, NP)),
+            D((8,)),
+            D((8,)),
+            D((T,)),
+            D((T,)),
+            D((T,)),
+            D((T,)),
+            D((T,)),
+            D((T,)),
+            D((T,)),
+            D((T,)),
+            D((T,)),
+            D((T,)),
+            D((T,)),
+            D((T,)),
+            D((T,)),
+            D((T,)),
         ],
         compiler_params=pltpu.CompilerParams(collective_id=0, has_side_effects=True, vmem_limit_bytes=LIMIT),
         name="block",

time: 55.6 us -> 50.8 us (0.914)
  Pallas kernels: 54.9 us -> 50.1 us
    pallas_call x1, Pallas kernels: 52.1 us -> 47.4 us  [step(): pl.pallas_call(functools.partial(kernel, sizes, H), out_shape=(HELD((B, H...]
where the time goes in v4:
time: 50.8 us; the launch traced here: 50.7 us
  Pallas kernels  50.1 us (99%)
  between operations  0.64 us (1%)
    pallas_call x1, Pallas kernels, step(): pl.pallas_call(functools.partial(kernel, sizes, H), out_shape=(HELD((B, H...  47.4 us
    pallas_call x1, Pallas kernels, step(): pl.pallas_call(write_out, out_shape=(jax.ShapeDtypeStruct((B, H, W, C), b...  2.73 us

profile of v4, /device:TPU:1, one launch (start us, length us, event | category | flops | bytes accessed | tf_op | source)
XLA Modules:
  0.0 50.7 jit_solution(3504096205081270309)
XLA Ops:
  0.6 47.4 %block.1 = (bf16[2,64,8,320]{3,2,1,0:T(8,128)(2,1)S(1)}, f32[2,64,8,320]{3,2,1,0:T(8,128)S(1)}, f32[3,3,40,320]{3,2,1,0:T(8,128)S(1)}, f32[8,320]{1,0:T(8,128)S(1)}, f32[320,1280]{1,0:T(8,128)S(1)}) custom-call(s32[2]{0:T(128)} %ts_hbm.1, f32[320]{0:T(512)} %gain_hbm.1, f32[320]{0:T(512)} %bias_hbm.1, f32[320]{0:T(512)} %cb_hbm.1, ...), custom_call_target="tpu_custom_call" | custom-call | tf_op jit(solution)/shard_map/block/pallas_call | solution.py:589
  48.0 2.7 %write_out.1 = (bf16[2,64,8,320]{3,2,1,0:T(8,128)(2,1)}, f32[2,64,8,320]{3,2,1,0:T(8,128)}, f32[3,3,40,320]{3,2,1,0:T(8,128)}, f32[320,1280]{1,0:T(8,128)}, f32[320]{0:T(512)}, /*index=5*/f32[320]{0:T(512)}, f32[320]{0:T(512)}) custom-call(bf16[2,64,8,320]{3,2,1,0:T(8,128)(2,1)S(1)} %get-tuple-element.19.ob, f32[2,64,8,320]{3,2,1,0:T(8,128)S(1)} %get-tuple-element.20.og, ...), custom_call_target="tpu_custom_call" | custom-call | tf_op jit(solution)/shard_map/write_out/pallas_call | solution.py:672
